TPU v7x, 32 devices: a whole 2x2x4 slice. The times are simulated.
32 devices in a mesh: parts: 2 (over x), rows: 16 (over z, y, core).
Axes of the slice: x: 2, y: 2, z: 4, core: 2. Of those that a mesh axis runs over, the one named last changes fastest.
Arguments:
- feature_bin: int32 [16384, 700], P(('parts', 'rows')), parts along dimension 0, may hold values from 0 to 255
- doc_leaf: int32 [16384], P(('parts', 'rows')), parts along dimension 0, may hold values from 0 to 31
- current_score: float32 [16384], P(('parts', 'rows')), parts along dimension 0, may hold values from -8 to 8
- relevance: int32 [16384], P(('parts', 'rows')), parts along dimension 0, may hold values from 0 to 4
- doc_rank: int32 [16384], P(('parts', 'rows')), parts along dimension 0, may hold values from 0 to 255, as said below
- query_length: int32 [64], P(('parts', 'rows')), parts along dimension 0, may hold values from 10 to 256, as said below
- feature_votes: int32 [32, 32, 20], P(('parts', 'rows')), parts along dimension 0, may hold values from 0 to 699, all different within a row
- elected: int32 [64, 40], P('parts'), parts along dimension 0, may hold values from 0 to 699, all different within a row
Outputs:
- gradient: float32 [16384], P(('parts', 'rows')), parts along dimension 0
- hessian: float32 [16384], P(('parts', 'rows')), parts along dimension 0
- vote_count: int32 [64, 700], P('parts'), parts along dimension 0
- split_gain: float32 [64, 40, 256], P('parts'), parts along dimension 0
There are 2 independent parts, one for each index of `parts`. A program takes and returns all parts, laid end to end along the dimension named above; each array names one. Nothing has to cross between parts.
Inputs may be any that keep to these rules, and one draw needn't show every extreme that they name: `query_length`: query q holds slots q * 256 to (q + 1) * 256 - 1 of the document arrays; in every draw some query has exactly 256 documents. `doc_rank`: within each query the live documents hold positions 0 to query_length - 1, each once; slots that are not live hold positions from query_length to 255. `feature_votes`: the 20 votes of one device for one leaf are different features. The 40 elected features of one leaf are different.
All inputs are finite; a program needn't handle non-finite values.
Results may differ from a plain program's by a relative error of at most 0.0003.
Values sent between devices are 32-bit elements; how exact they have to be, the bound alone decides.
No kernel may reach another device: no remote copies, remote signals or barrier semaphores. Data moves between devices by JAX's collectives and lax.ppermute only.
A program may use at most 64 MiB of HBM per device.

v0:
```python
import math

import jax
import jax.numpy as jnp
from jax import lax
from jax.sharding import PartitionSpec as P

B = 256
QMAX = 256


ridge_weight = 1.0


def query_terms(scores, levels, places, length):
    positions = jnp.arange(scores.shape[0], dtype=jnp.int32)
    living = positions < length
    gains = jnp.exp2(levels.astype(jnp.float32)) - 1.0
    discount = 1.0 / jnp.log2(places.astype(jnp.float32) + 2.0)
    higher = (levels[None, :] > levels[:, None]) & living[None, :]
    earlier = (
        (levels[None, :] == levels[:, None])
        & (positions[None, :] < positions[:, None])
        & living[None, :]
    )
    ideal_place = jnp.sum((higher | earlier).astype(jnp.float32), axis=1)
    ideal = jnp.sum(jnp.where(living, gains / jnp.log2(ideal_place + 2.0), 0.0))
    scaling = 1.0 / jnp.maximum(ideal, 1.0)
    ordered = (levels[:, None] > levels[None, :]) & living[:, None] & living[None, :]
    chance = jax.nn.sigmoid(scores[None, :] - scores[:, None])
    change = (
        (gains[:, None] - gains[None, :]) * jnp.abs(discount[:, None] - discount[None, :]) * scaling
    )
    pushes = jnp.where(ordered, chance * change, 0.0)
    curves = jnp.where(ordered, chance * (1.0 - chance) * change, 0.0)
    return (
        jnp.sum(pushes, axis=0) - jnp.sum(pushes, axis=1),
        jnp.sum(curves, axis=0) + jnp.sum(curves, axis=1),
    )


def build_histogram(feature_bin, doc_leaf, gradient, hessian, elected, bins):
    leaves, picked = elected.shape
    documents = feature_bin.shape[0]
    leaf_hot = (doc_leaf[:, None] == jnp.arange(leaves, dtype=jnp.int32)[None, :]).astype(
        jnp.float32
    )
    columns = jnp.dot(
        leaf_hot, elected.astype(jnp.float32), precision=lax.Precision.HIGHEST
    ).astype(jnp.int32)
    chosen = jnp.take_along_axis(feature_bin, columns, axis=1)
    weighted = jnp.concatenate([leaf_hot * gradient[:, None], leaf_hot * hessian[:, None]], axis=1)
    block_rows = math.gcd(documents, 512)
    block_count = documents // block_rows
    bin_ids = jnp.arange(bins, dtype=jnp.int32)

    def add_block(index, total):
        onehot = (chosen[:, :, None] == bin_ids[None, None, :]).astype(jnp.float32)
        onehot = onehot.reshape(block_rows, picked * bins)
        return total + jnp.dot(weighted.T, onehot, precision=lax.Precision.HIGHEST)

    empty = jnp.zeros((2 * leaves, picked * bins), jnp.float32)
    total = lax.fori_loop(0, block_count, add_block, empty)
    return total.reshape(2, leaves, picked, bins)


def split_score(prefix, whole):
    remain = whole - prefix
    return (
        prefix[0] * prefix[0] / (prefix[1] + ridge_weight)
        + remain[0] * remain[0] / (remain[1] + ridge_weight)
        - whole[0] * whole[0] / (whole[1] + ridge_weight)
    )


def count_votes(feature_votes, features):
    hits = feature_votes[..., None] == jnp.arange(features, dtype=jnp.int32)
    return jnp.sum(hits.astype(jnp.int32), axis=(0, 2))


def on_device(
    feature_bin, doc_leaf, current_score, relevance, doc_rank, query_length, feature_votes, elected
):
    features = feature_bin.shape[1]
    all_votes = lax.all_gather(feature_votes, "rows", axis=0, tiled=True)
    vote_count = count_votes(all_votes, features)

    def one_query(items):
        return query_terms(items[0], items[1], items[2], items[3])

    gradient, hessian = lax.map(
        one_query,
        (
            current_score.reshape(-1, QMAX),
            relevance.reshape(-1, QMAX),
            doc_rank.reshape(-1, QMAX),
            query_length,
        ),
    )
    gradient = gradient.reshape(-1)
    hessian = hessian.reshape(-1)
    histogram = build_histogram(feature_bin, doc_leaf, gradient, hessian, elected, B)
    summed = lax.psum(histogram, "rows")
    prefix = jnp.cumsum(summed, axis=3)
    whole = jnp.sum(summed, axis=3, keepdims=True)
    split_gain = split_score(prefix, whole)
    return (gradient, hessian, vote_count, split_gain)


def solution(mesh):
    return jax.shard_map(
        on_device,
        mesh=mesh,
        in_specs=(
            P(("parts", "rows"), None),
            P(("parts", "rows")),
            P(("parts", "rows")),
            P(("parts", "rows")),
            P(("parts", "rows")),
            P(("parts", "rows")),
            P(("parts", "rows"), None, None),
            P("parts", None),
        ),
        out_specs=(
            P(("parts", "rows")),
            P(("parts", "rows")),
            P("parts", None),
            P("parts", None, None),
        ),
        check_vma=False,
    )
```

profile of v0, /device:TPU:0, one launch (start us, length us, event | category | flops | bytes accessed | tf_op | source)
XLA Modules:
  0.0 409.0 jit_solution(16073954382203800596)
XLA Ops:
  7.2 0.0 copy-start
  7.2 0.0 all-reduce.2.cloned.1.call-start
  7.3 0.8 reshape.169
  8.0 0.7 reshape.170
  8.7 0.7 reshape.171
  9.4 9.2 %while.18 = (s32[]{:T(128)}, f32[2,256]{1,0:T(2,128)S(1)}, f32[2,256]{1,0:T(2,128)S(1)}, s32[2,256]{1,0:T(2,128)S(1)}, s32[2]{0:T(128)}, /*index=5*/f32[2,256]{1...) while((s32[]{:T(128)}, f32[2,256]{1,0:T(2,128)S(1)}, f32[2,256]{1,0:T(2,128)S(1)}, ...), condition=%wide.region_7.8_spmd, body=%wide.region_0.7_spmd.sunk | while | flops 2035203 | bytes 32681 | solution.py:91
  9.5 1.2 dynamic_slice.34
  10.7 0.6 iota_compare_fusion.6
  11.4 0.2 convert_reduce_fusion.3
  11.6 1.3 exponential_add_fusion.5
  13.5 0.4 fusion.28
  14.1 1.2 dynamic_slice.34
  15.3 0.6 iota_compare_fusion.6
  16.0 0.2 convert_reduce_fusion.3
  16.2 1.3 exponential_add_fusion.5
  18.2 0.4 fusion.28
  18.6 0.0 copy-start.3
  18.7 0.0 copy-start.4
  18.7 1.0 bitcast_or_fusion
  19.7 0.1 copy.34
  19.8 0.2 reshape.179
  20.0 163.1 %gather_fusion = s32[20480]{0:T(1024)S(1)} fusion(s32[512,700]{0,1:T(8,128)S(1)} %copy-done, s32[20480]{0:T(1024)S(1)} %reshape.179), kind=kCustom, calls=%fused_computation | custom fusion | bytes 327680 | tf_op jit(solution)/shard_map/jit(take_along_axis)/gather | solution.py:51
  183.1 0.2 reshape.182
  183.3 0.1 copy.35
  183.5 3.3 bitcast_compare_fusion
  186.8 11.0 %fusion.22 = f32[2,32,40,256]{3,1,2,0:T(8,128)} fusion(f32[2,32,512,1]{2,1,3,0:T(8,128)S(1)} %bitcast.69, pred[40,256,512,1]{2,1,0,3:T(32,128)(4,1)S(1)} %bitcast.68), kind=kOutput, calls=%fused_computation.56 | convolution fusion | flops 4026531840 | bytes 7995392 | tf_op jit(solution)/shard_map/while/body/eval_jaxpr/dot_general | solution.py:60
  197.9 0.0 all-reduce.2.cloned.1.call-update
  197.9 0.7 copy-done.2
  198.6 24.5 %all_gather.3 = s32[16,32,20]{1,2,0:T(8,128)S(1)} all-gather(s32[1,32,20]{1,2,0:T(8,128)S(1)} %copy.33), channel_id=1, replica_groups=mesh['parts'=2,'rows'=16] {'rows'}, dimensions={0}, use_global_device_ids=true | all-gather | bytes 43520 | tf_op jit(solution)/shard_map/all_gather | solution.py:85
  223.1 4.4 %convert_reduce_fusion.1 = s32[32,700]{1,0:T(8,128)} fusion(s32[16,32,20]{1,2,0:T(8,128)S(1)} %all_gather.3), kind=kLoop, calls=%fused_computation.25 | loop fusion | flops 21481600 | bytes 130560 | tf_op jit(solution)/shard_map/reduce_sum | solution.py:78
  227.5 74.4 %all-reduce.2.cloned.1.call-done = f32[2,32,40,256]{3,1,2,0:T(8,128)} async-done(((f32[2,32,40,256]{3,1,2,0:T(8,128)}), f32[2,32,40,256]{3,1,2,0:T(8,128)}) %all-reduce.2.cloned.1.call-update) | async-done | bytes 2621456 | tf_op jit(solution)/shard_map/psum | solution.py:103
  302.0 2.2 reduce_sum.91
  304.1 0.1 copy.40
  304.2 4.3 %reshape.175 = f32[2,32,40,2,128]{4,3,1,2,0:T(2,128)} reshape(f32[2,32,40,256]{3,1,2,0:T(8,128)} %all-reduce.2.cloned.1.call-done) | data formatting | bytes 5242880 | tf_op jit(solution)/shard_map/reshape.2
  308.5 4.8 %copy.36 = f32[2,32,40,2,128]{4,2,3,1,0:T(8,128)} copy(f32[2,32,40,2,128]{4,3,1,2,0:T(2,128)} %reshape.175) | data formatting | bytes 5242880 | tf_op jit(solution)/shard_map/reshape.2
  313.3 69.9 %reduce-window.6 = f32[2,32,40,2,128]{4,2,3,1,0:T(8,128)} reduce-window(f32[2,32,40,2,128]{4,2,3,1,0:T(8,128)} %copy.36, f32[]{:T(128)} %constant.79.clone.1), window={size=1x1x1x1x128 pad=0_0x0_0x0_0x0_0x127_0}, to_apply=%region_10.11 | reduce-window | flops 83230720 | bytes 5242884 | tf_op jit(solution)/shard_map/reduce-window
  383.1 4.0 slice.41
  387.1 2.7 copy.37
  389.8 0.2 fusion.14
  390.0 0.1 copy.38
  390.0 2.3 broadcast_add_fusion
  392.4 0.2 copy-done.1
  392.5 2.3 bitcast_subtract_fusion
  394.8 0.2 fusion.13
  395.0 1.7 copy.39
  396.7 2.3 div.58
  399.1 0.1 copy.42
  399.1 3.1 fusion.12
  (31 shorter events, 0.3 us)
Async XLA Ops:
  7.2 12.8 %copy-start = (s32[512,700]{0,1:T(8,128)S(1)}, s32[512,700]{0,1:T(8,128)}, u32[]{:S(2)}) copy-start(s32[512,700]{0,1:T(8,128)} %param.10) | copy-start | bytes 4300804
  7.2 294.8 %all-reduce.2.cloned.1.call-start = ((), (), s32[]{:S(2)}) async-start(), calls=%async_computation | async-start | bytes 5242880 | tf_op jit(solution)/shard_map/psum | solution.py:103
  18.6 164.8 %copy-start.3 = (f32[1,2,2,128]{3,1,2,0:T(2,128)}, f32[1,2,2,128]{3,1,2,0:T(2,128)S(1)}, u32[]{:S(2)}) copy-start(f32[1,2,2,128]{3,1,2,0:T(2,128)S(1)} %copy.45) | copy-start | bytes 6148
  18.7 164.8 %copy-start.4 = (f32[1,2,2,128]{3,1,2,0:T(2,128)}, f32[1,2,2,128]{3,1,2,0:T(2,128)S(1)}, u32[]{:S(2)}) copy-start(f32[1,2,2,128]{3,1,2,0:T(2,128)S(1)} %copy.46) | copy-start | bytes 6148
  20.0 163.4 %copy-start.5 = (s32[512]{0:T(512)S(1)}, s32[512]{0:T(512)}, u32[]{:S(2)}) copy-start(s32[512]{0:T(512)} %param.11) | copy-start | bytes 6148
  197.9 0.7 copy-start.2
  390.0 2.5 copy-start.1
Sparse Core Ops, SparseCore 0:
  198.0 103.8 all-reduce.1
where the time goes:
time: 417 us; the launch traced here: 409 us
  local copies, waits for them, and re-layouts  189 us (45%)
  other arithmetic  92.9 us (22%)
  waiting for transfers between devices  74.4 us (18%)
  blocking collectives  24.5 us (6%)
  between operations  14.3 us (3%)
  matrix products  12 us (3%)
    gather x5, local copies, waits for them, and re-layouts, build_histogram(): chosen = jnp.take_along_axis(feature_bin, columns, axis=1)  164 us
    psum x1, waiting for transfers between devices, on_device(): summed = lax.psum(histogram, 'rows')  74.4 us
    another operation x5, other arithmetic  72.3 us
    all_gather x1, blocking collectives, on_device(): all_votes = lax.all_gather(feature_votes, 'rows', axis=0, tiled=True)  24.5 us
    dot_general x1, matrix products, add_block(): return total + jnp.dot(weighted.T, onehot, precision=lax.Precision.HIGHEST)  11 us
    another operation x4, local copies, waits for them, and re-layouts  9.1 us
  transfers between devices with their start and end apart: 1, of which 1 were waited for; matrix products, arithmetic and copies ran while one was open for 1% of the time, Pallas kernels for 0%

commit v1 on v0

v1 whole, which is shorter than its diff:
```python
import jax
import jax.numpy as jnp
from jax import lax
from jax.experimental import pallas as pl
from jax.experimental.pallas import tpu as pltpu
from jax.sharding import PartitionSpec as P

B = 256
LANES = 128
HALVES = B // LANES
LEVELS = 4

ridge_weight = 1.0


def cdiv(a, b):
    return -(-a // b)


def round_up(a, b):
    return cdiv(a, b) * b


def query_rows(score, level, rank, lengths, slots):
    documents = score.shape[1]
    queries = documents // slots
    gain = jnp.left_shift(1, level).astype(jnp.float32) - 1.0
    discount = 1.0 / jnp.log2(rank.astype(jnp.float32) + 2.0)
    place = lax.broadcasted_iota(jnp.int32, (1, slots), 1)
    place_discount = 1.0 / jnp.log2(place.astype(jnp.float32) + 2.0)
    gradients = []
    hessians = []
    for q in range(queries):
        lanes = slice(q * slots, (q + 1) * slots)
        live = place < lengths[q]
        live_row = live.astype(jnp.float32)
        score_row = score[:, lanes]
        gain_row = gain[:, lanes]
        discount_row = discount[:, lanes]
        level_row = jnp.where(live, level[:, lanes], -1)
        ideal_gain = jnp.zeros((1, slots), jnp.float32)
        for v in range(1, LEVELS + 1):
            count = jnp.sum((level_row >= v).astype(jnp.float32), axis=1, keepdims=True)
            ideal_gain = ideal_gain + jnp.where(
                place.astype(jnp.float32) < count, float(2 ** (v - 1)), 0.0
            )
        ideal = jnp.sum(ideal_gain * place_discount, axis=1, keepdims=True)
        scaling = 1.0 / jnp.maximum(ideal, 1.0)
        rows = jnp.concatenate(
            [score_row, gain_row, discount_row, live_row, jnp.zeros((4, slots), jnp.float32)],
            axis=0,
        )
        columns = rows.T
        step = 32
        push_sum = jnp.zeros((8, slots), jnp.float32)
        curve_sum = jnp.zeros((8, slots), jnp.float32)
        for r in range(0, slots, step):
            part = columns[r : r + step]
            gap = (part[:, 1:2] - gain_row) * part[:, 3:4]
            change = gap * jnp.abs(part[:, 2:3] - discount_row)
            lead = score_row - part[:, 0:1]
            chance = 1.0 / (1.0 + jnp.exp(jnp.where(gap > 0.0, -lead, lead)))
            push = chance * change
            curve = (1.0 - chance) * jnp.abs(push)
            for k in range(0, step, 8):
                push_sum = push_sum + push[k : k + 8]
                curve_sum = curve_sum + curve[k : k + 8]
        factor = scaling * live_row
        gradients.append(jnp.sum(push_sum, axis=0, keepdims=True) * factor)
        hessians.append(jnp.sum(curve_sum, axis=0, keepdims=True) * factor)
    return jnp.concatenate(gradients, axis=1), jnp.concatenate(hessians, axis=1)


def local_stage(bins, leaf, score, level, rank, lengths, votes, elected, plan):
    features, documents = bins.shape
    leaves, picked = elected.shape
    kept = votes.shape[1]
    padded = round_up(picked, 8)
    slots = documents // lengths.shape[0]
    group = 8 if leaves % 8 == 0 else leaves
    per_row = LANES // leaves

    def body(bins_ref, leaf_ref, score_ref, level_ref, rank_ref, length_ref, votes_ref,
             elected_ref, grad_ref, hess_ref, packet_ref, square, chosen_ref):
        square[...] = jnp.zeros(square.shape, jnp.float32)
        square[0:leaves, 0:picked] = elected_ref[...].astype(jnp.float32)
        elected_t = square[...].T
        square[...] = jnp.zeros(square.shape, jnp.float32)
        square[0:leaves, 0:kept] = votes_ref[...].astype(jnp.float32)
        votes_t = square[...].T
        table = bins_ref[...].astype(jnp.float32).astype(jnp.bfloat16)
        leaf_row = leaf_ref[...]
        feature = lax.broadcasted_iota(jnp.int32, (padded, features), 1).astype(jnp.float32)
        chosen = jnp.zeros((padded, documents), jnp.float32)
        for first in range(0, leaves, group):
            picks = []
            for l in range(first, first + group):
                picks.append((elected_t[0:padded, l : l + 1] == feature).astype(jnp.float32))
            hot = jnp.concatenate(picks, axis=0).astype(jnp.bfloat16)
            found = jnp.dot(hot, table, preferred_element_type=jnp.float32)
            for i in range(group):
                chosen = jnp.where(
                    leaf_row == first + i, found[i * padded : (i + 1) * padded], chosen
                )
        chosen_ref[...] = chosen
        gradient, hessian = query_rows(
            score_ref[...], level_ref[...], rank_ref[...], length_ref, slots
        )
        grad_ref[...] = gradient
        hess_ref[...] = hessian
        vote_parts = []
        for k0 in range(0, kept, per_row):
            part = votes_t[k0 : k0 + 1]
            for i in range(1, min(per_row, kept - k0)):
                part = part + pltpu.roll(votes_t[k0 + i : k0 + i + 1], i * leaves, 1)
            vote_parts.append(part)
        while len(vote_parts) * LANES % documents:
            vote_parts.append(jnp.zeros((1, LANES), jnp.float32))
        per = documents // LANES
        shared = [leaf_row.astype(jnp.float32), gradient, hessian]
        for r in range(plan["vote_rows"]):
            shared.append(jnp.concatenate(vote_parts[r * per : (r + 1) * per], axis=1))
        spare = plan["rows"] - plan["picks"] - len(shared)
        if spare:
            shared.append(jnp.zeros((spare, documents), jnp.float32))
        shared = jnp.concatenate(shared, axis=0)
        for j in range(plan["devices"]):
            start = min(j * plan["units"] // HALVES, padded - plan["picks"])
            packet_ref[j, 0 : plan["picks"], :] = chosen_ref[start : start + plan["picks"], :]
            packet_ref[j, plan["picks"] :, :] = shared

    vmem = pl.BlockSpec(memory_space=pltpu.VMEM)
    return pl.pallas_call(
        body,
        in_specs=[vmem] * 5 + [pl.BlockSpec(memory_space=pltpu.SMEM)] + [vmem] * 2,
        out_specs=[vmem] * 3,
        out_shape=[
            jax.ShapeDtypeStruct((1, documents), jnp.float32),
            jax.ShapeDtypeStruct((1, documents), jnp.float32),
            jax.ShapeDtypeStruct((plan["devices"], plan["rows"], documents), jnp.float32),
        ],
        scratch_shapes=[
            pltpu.VMEM((LANES, LANES), jnp.float32),
            pltpu.VMEM((padded, documents), jnp.float32),
        ],
        name="local_stage",
    )(bins, leaf, score, level, rank, lengths, votes, elected)


def gain_stage(packets, where, leaves, plan):
    devices, rows, documents = packets.shape
    picks = plan["picks"]
    units = plan["units"]
    chunk = 4 if devices % 4 == 0 else 1

    def body(where_ref, packet_ref, out_ref):
        base = where_ref[0] * units
        first_pick = base // HALVES
        first_pick = jnp.minimum(first_pick, plan["padded"] - picks)
        leaf_id = lax.broadcasted_iota(jnp.int32, (leaves, documents), 0).astype(jnp.float32)
        bin_id = lax.broadcasted_iota(jnp.int32, (LANES, documents), 0).astype(jnp.float32)
        local = []
        shift = []
        for i in range(units):
            local.append(jnp.clip((base + i) // HALVES - first_pick, 0, picks - 1))
            shift.append((((base + i) % HALVES) * LANES).astype(jnp.float32))
        total = jnp.zeros((4 * leaves, units * LANES), jnp.float32)
        grad_all = jnp.zeros((leaves, documents), jnp.float32)
        hess_all = jnp.zeros((leaves, documents), jnp.float32)
        for s0 in range(0, devices, chunk):
            weights = []
            steps = [[] for _ in range(units)]
            for s in range(s0, s0 + chunk):
                mine = packet_ref[s, picks : picks + 1, :] == leaf_id
                grad = jnp.where(mine, packet_ref[s, picks + 1 : picks + 2, :], 0.0)
                hess = jnp.where(mine, packet_ref[s, picks + 2 : picks + 3, :], 0.0)
                grad_all = grad_all + grad
                hess_all = hess_all + hess
                grad_high = grad.astype(jnp.bfloat16)
                hess_high = hess.astype(jnp.bfloat16)
                grad_low = (grad - grad_high.astype(jnp.float32)).astype(jnp.bfloat16)
                hess_low = (hess - hess_high.astype(jnp.float32)).astype(jnp.bfloat16)
                weights.append(
                    jnp.concatenate([grad_high, hess_high, grad_low, hess_low], axis=0)
                )
                for i in range(units):
                    value = packet_ref[s, pl.ds(local[i], 1), :] - shift[i]
                    steps[i].append((value <= bin_id).astype(jnp.float32).astype(jnp.bfloat16))
            weight = jnp.concatenate(weights, axis=1)
            step = jnp.concatenate([jnp.concatenate(p, axis=1) for p in steps], axis=0)
            total = total + lax.dot_general(
                weight, step, (((1,), (1,)), ((), ())), preferred_element_type=jnp.float32
            )
        prefix_grad = total[0:leaves] + total[2 * leaves : 3 * leaves]
        prefix_hess = total[leaves : 2 * leaves] + total[3 * leaves :]
        whole_grad = jnp.sum(grad_all, axis=1, keepdims=True)
        whole_hess = jnp.sum(hess_all, axis=1, keepdims=True)
        rest_grad = whole_grad - prefix_grad
        rest_hess = whole_hess - prefix_hess
        gains = (
            prefix_grad * prefix_grad / (prefix_hess + ridge_weight)
            + rest_grad * rest_grad / (rest_hess + ridge_weight)
            - whole_grad * whole_grad / (whole_hess + ridge_weight)
        )
        for i in range(units):
            out_ref[i * leaves : (i + 1) * leaves, :] = gains[:, i * LANES : (i + 1) * LANES]

    vmem = pl.BlockSpec(memory_space=pltpu.VMEM)
    return pl.pallas_call(
        body,
        in_specs=[pl.BlockSpec(memory_space=pltpu.SMEM), vmem],
        out_specs=vmem,
        out_shape=jax.ShapeDtypeStruct((units * leaves, LANES), jnp.float32),
        name="gain_stage",
    )(where, packets)


def vote_stage(packets, features, leaves, kept, plan):
    devices, rows, documents = packets.shape
    first_row = plan["picks"] + 3
    lines = cdiv(kept * leaves, LANES)
    per = documents // LANES
    padded = round_up(features, 8)
    step = 64

    def body(packet_ref, out_ref, count):
        lane = lax.broadcasted_iota(jnp.int32, (1, LANES), 1)

        def block(index, carry):
            start = pl.multiple_of(index * step, step)
            feature = (lax.broadcasted_iota(jnp.int32, (step, LANES), 0) + start).astype(
                jnp.float32
            )
            total = jnp.zeros((step, LANES), jnp.float32)
            for s in range(devices):
                for line in range(lines):
                    row = first_row + line // per
                    col = (line % per) * LANES
                    values = packet_ref[s, row : row + 1, col : col + LANES]
                    inside = kept * leaves - line * LANES
                    if inside < LANES:
                        values = jnp.where(lane < inside, values, -1.0)
                    total = total + (values == feature).astype(jnp.float32)
            count[pl.ds(start, step), :] = total
            return carry

        lax.fori_loop(0, cdiv(padded, step), block, 0)
        turned = count[...].T
        summed = turned[0:leaves]
        for i in range(1, LANES // leaves):
            summed = summed + turned[i * leaves : (i + 1) * leaves]
        out_ref[...] = summed[:, 0:features].astype(jnp.int32)

    vmem = pl.BlockSpec(memory_space=pltpu.VMEM)
    depth = round_up(round_up(padded, step), LANES)
    return pl.pallas_call(
        body,
        in_specs=[vmem],
        out_specs=vmem,
        out_shape=jax.ShapeDtypeStruct((leaves, features), jnp.int32),
        scratch_shapes=[pltpu.VMEM((depth, LANES), jnp.float32)],
        name="vote_stage",
    )(packets)


def place_stage(blocks, where, leaves, picked, plan):
    units = plan["units"]

    def body(where_ref, block_ref, out_ref):
        here = where_ref[0]
        for unit in range(picked * HALVES):
            slot = unit // units
            if plan["bits"]:
                offset = here ^ slot
                slot = 0
                for position, bit in enumerate(plan["bits"]):
                    slot = slot + jnp.where((offset & bit) != 0, 1 << position, 0)
            start = pl.multiple_of((slot * units + unit % units) * leaves, leaves)
            lane = (unit % HALVES) * LANES
            out_ref[:, unit // HALVES, lane : lane + LANES] = block_ref[pl.ds(start, leaves), :]

    vmem = pl.BlockSpec(memory_space=pltpu.VMEM)
    return pl.pallas_call(
        body,
        in_specs=[pl.BlockSpec(memory_space=pltpu.SMEM), vmem],
        out_specs=vmem,
        out_shape=jax.ShapeDtypeStruct((leaves, picked, B), jnp.float32),
        name="place_stage",
    )(where, blocks)


def solution(mesh):
    devices = mesh.shape["rows"]

    def on_device(
        feature_bin, doc_leaf, current_score, relevance, doc_rank, query_length, feature_votes,
        elected,
    ):
        documents, features = feature_bin.shape
        leaves, picked = elected.shape
        kept = feature_votes.shape[2]
        units = cdiv(picked * HALVES, devices)
        padded = round_up(picked, 8)
        picks = max(
            (j * units + units - 1) // HALVES - (j * units) // HALVES + 1 for j in range(devices)
        )
        vote_rows = cdiv(kept * leaves, documents)
        plan = {
            "devices": devices,
            "units": units,
            "picks": picks,
            "padded": padded,
            "vote_rows": vote_rows,
            "rows": round_up(picks + 3 + vote_rows, 8),
            "bits": None,
        }
        where = lax.axis_index("rows").astype(jnp.int32).reshape(1)
        gradient, hessian, packets = local_stage(
            feature_bin.T,
            doc_leaf.reshape(1, -1),
            current_score.reshape(1, -1),
            relevance.reshape(1, -1),
            doc_rank.reshape(1, -1),
            query_length,
            feature_votes.reshape(leaves, kept),
            elected,
            plan,
        )
        received = lax.all_to_all(packets, "rows", 0, 0)
        block = gain_stage(received, where, leaves, plan)
        vote_count = vote_stage(received, features, leaves, kept, plan)
        if devices & (devices - 1) == 0 and devices > 1:
            gathered = block
            plan["bits"] = [1 << b for b in reversed(range(devices.bit_length() - 1))]
            for bit in plan["bits"]:
                other = lax.ppermute(gathered, "rows", [(i, i ^ bit) for i in range(devices)])
                gathered = jnp.concatenate([gathered, other], axis=0)
        else:
            gathered = lax.all_gather(block, "rows", axis=0, tiled=True)
        split_gain = place_stage(gathered, where, leaves, picked, plan)
        return gradient.reshape(-1), hessian.reshape(-1), vote_count, split_gain

    return jax.shard_map(
        on_device,
        mesh=mesh,
        in_specs=(
            P(("parts", "rows"), None),
            P(("parts", "rows")),
            P(("parts", "rows")),
            P(("parts", "rows")),
            P(("parts", "rows")),
            P(("parts", "rows")),
            P(("parts", "rows"), None, None),
            P("parts", None),
        ),
        out_specs=(
            P(("parts", "rows")),
            P(("parts", "rows")),
            P("parts", None),
            P("parts", None, None),
        ),
        check_vma=False,
    )
```

time: 417 us -> 63.7 us (0.15); the launches traced: 409 us -> 63.2 us
  local copies, waits for them, and re-layouts: 189 us -> 3.26 us
  other arithmetic: 92.9 us -> 2.74 us
  waiting for transfers between devices: 74.4 us -> 30.9 us
  blocking collectives: 24.5 us -> 0 us
  Pallas kernels: 0 us -> 16.9 us
  between operations: 14.3 us -> 0.73 us
  matrix products: 12 us -> 0 us
  starting transfers between devices: 0.04 us -> 8.69 us
    gather x5 -> x0, local copies, waits for them, and re-layouts: 164 us -> none  [build_histogram(): chosen = jnp.take_along_axis(feature_bin, columns, axis=1)]
    psum x1 -> x0, waiting for transfers between devices: 74.4 us -> none  [on_device(): summed = lax.psum(histogram, 'rows')]
    another operation x5 -> x0, other arithmetic: 72.3 us -> none
    all_gather x1 -> x0, blocking collectives: 24.5 us -> none  [on_device(): all_votes = lax.all_gather(feature_votes, 'rows', axis=0, tiled=True)]
    ppermute x0 -> x4, waiting for transfers between devices: none -> 20.9 us  [on_device(): lax.ppermute(gathered, 'rows', [(i, i ^ bit) for i in range(devices)])]
    pallas_call x0 -> x4, Pallas kernels: none -> 16.9 us  [the longest x1 5.05 us: vote_stage(): pl.pallas_call(body, in_specs=[vmem], out_specs=vmem, out_shape=jax.Shape...]
    dot_general x2 -> x0, matrix products: 12 us -> none  [the longest x1 11 us: add_block(): return total + jnp.dot(weighted.T, onehot, precision=lax.Precision.HIGHEST)]
    all_to_all x0 -> x1, waiting for transfers between devices: none -> 10 us  [on_device(): received = lax.all_to_all(packets, 'rows', 0, 0)]
  transfers between devices with their start and end apart: 1 -> 5, of which waited for: 1 -> 4; matrix products, arithmetic and copies ran while one was open for 1% -> 0% of each run, Pallas kernels for 0% -> 8%
where the time goes in v1:
time: 63.7 us; the launch traced here: 63.2 us
  waiting for transfers between devices  30.9 us (49%)
  Pallas kernels  16.9 us (27%)
  starting transfers between devices  8.69 us (14%)
  local copies, waits for them, and re-layouts  3.26 us (5%)
  other arithmetic  2.74 us (4%)
  between operations  0.73 us (1%)
    ppermute x4, waiting for transfers between devices, on_device(): lax.ppermute(gathered, 'rows', [(i, i ^ bit) for i in range(devices)])  20.9 us
    all_to_all x1, waiting for transfers between devices, on_device(): received = lax.all_to_all(packets, 'rows', 0, 0)  10 us
    all_to_all x1, starting transfers between devices, on_device(): received = lax.all_to_all(packets, 'rows', 0, 0)  7.41 us
    pallas_call x1, Pallas kernels, vote_stage(): pl.pallas_call(body, in_specs=[vmem], out_specs=vmem, out_shape=jax.Shape...  5.05 us
    pallas_call x1, Pallas kernels, gain_stage(): pl.pallas_call(body, in_specs=[pl.BlockSpec(memory_space=pltpu.SMEM), vme...  4.97 us
    pallas_call x1, Pallas kernels, local_stage(): pl.pallas_call(body, in_specs=[vmem] * 5 + [pl.BlockSpec(memory_space=plt...  3.71 us
    unnamed x11, local copies, waits for them, and re-layouts  3.22 us
    pallas_call x1, Pallas kernels, place_stage(): pl.pallas_call(body, in_specs=[pl.BlockSpec(memory_space=pltpu.SMEM), vme...  3.14 us
  transfers between devices with their start and end apart: 5, of which 4 were waited for; matrix products, arithmetic and copies ran while one was open for 0% of the time, Pallas kernels for 8%

profile of v1, /device:TPU:0, one launch (start us, length us, event | category | flops | bytes accessed | tf_op | source)
XLA Modules:
  0.0 63.2 jit_solution(16654418049464959217)
XLA Ops:
  0.6 1.4 %copy.12 = s32[1,32,20]{2,1,0:T(8,128)} copy(s32[1,32,20]{1,0,2:T(1,128)} %param.14) | data formatting | bytes 5120 | tf_op args[6]
  2.0 3.7 %local_stage.1 = (f32[1,512]{1,0:T(1,128)}, f32[1,512]{1,0:T(1,128)}, f32[16,8,512]{2,1,0:T(8,128)}) custom-call(s32[700,512]{1,0:T(8,128)} %bitcast.9, s32[1,512]{1,0:T(1,128)} %bitcast.11, f32[1,512]{1,0:T(1,128)} %bitcast.12, s32[1,512]{1,0:T(1,128)} %bitcast.13, s32[1,512]{1,0:T(1,128)} %bitcast.14, s32[2]{0:T(128)} %length_ref.1, s32[32,20]{1,0:T(8,128)} %bitcast.10, ...), custom_call_target="tpu_custom_call" | custom-call | tf_op jit(solution)/shard_map/local_stage/pallas_call | solution.py:133
  5.7 7.4 %all-to-all-start = ((f32[16,8,512]{2,1,0:T(8,128)}), f32[16,8,512]{2,1,0:T(8,128)S(1)}, u32[]{:S(2)}, u32[]{:S(2)}) async-start(f32[16,8,512]{2,1,0:T(8,128)} %get-tuple-element.9), calls=%async_computation | async-start | bytes 524288 | tf_op jit(solution)/shard_map/all_to_all | solution.py:329
  13.1 10.0 %all-to-all-done.packet_ref = f32[16,8,512]{2,1,0:T(8,128)S(1)} async-done(((f32[16,8,512]{2,1,0:T(8,128)}), f32[16,8,512]{2,1,0:T(8,128)S(1)}, u32[]{:S(2)}, u32[]{:S(2)}) %all-to-all-start) | async-done | bytes 262176 | tf_op jit(solution)/shard_map/all_to_all | solution.py:329
  23.2 0.0 copy-start
  23.2 0.7 %copy-done = f32[16,8,512]{2,1,0:T(8,128)} copy-done((f32[16,8,512]{2,1,0:T(8,128)}, f32[16,8,512]{2,1,0:T(8,128)S(1)}, u32[]{:S(2)}) %copy-start) | copy-done | bytes 262168
  23.9 5.0 %gain_stage.1 = f32[160,128]{1,0:T(8,128)} custom-call(s32[1]{0:T(128)} %bitcast.8.where_ref, f32[16,8,512]{2,1,0:T(8,128)} %copy-done), custom_call_target="tpu_custom_call" | custom-call | tf_op jit(solution)/shard_map/gain_stage/pallas_call | solution.py:209
  28.8 0.0 copy-start.1
  28.8 1.1 %collective-permute-start = (f32[160,128]{1,0:T(8,128)}, f32[160,128]{1,0:T(8,128)S(1)}, u32[]{:S(2)}, u32[]{:S(2)}) collective-permute-start(f32[160,128]{1,0:T(8,128)} %gain_stage.1), channel_id=1, source_target_pairs={{0,8},{1,9},{2,10},{3,11},{4,12},{5,13},{6,14},{7,15},{8,0},{9,1},... | collective-permute-start | bytes 245768 | tf_op jit(solution)/shard_map/ppermute | solution.py:336
  29.9 6.0 %collective-permute-done = f32[160,128]{1,0:T(8,128)S(1)} collective-permute-done((f32[160,128]{1,0:T(8,128)}, f32[160,128]{1,0:T(8,128)S(1)}, u32[]{:S(2)}, u32[]{:S(2)}) %collective-permute-start) | collective-permute-done | bytes 81952 | tf_op jit(solution)/shard_map/ppermute | solution.py:336
  35.9 0.9 %pad_maximum_fusion.2 = f32[320,128]{1,0:T(8,128)S(1)} fusion(f32[160,128]{1,0:T(8,128)S(1)} %collective-permute-done, f32[160,128]{1,0:T(8,128)} %gain_stage.1), kind=kLoop, calls=%fused_computation.2 | loop fusion | flops 40960 | bytes 327680 | tf_op jit(solution)/shard_map/concatenate | solution.py:337
  36.8 0.1 collective-permute-start.1
  36.9 6.1 %collective-permute-done.1 = f32[320,128]{1,0:T(8,128)S(1)} collective-permute-done((f32[320,128]{1,0:T(8,128)S(1)}, f32[320,128]{1,0:T(8,128)S(1)}, u32[]{:S(2)}, u32[]{:S(2)}) %collective-permute-start.1) | collective-permute-done | bytes 163872 | tf_op jit(solution)/shard_map/ppermute | solution.py:336
  43.0 0.9 %pad_maximum_fusion.1 = f32[640,128]{1,0:T(8,128)S(1)} fusion(f32[320,128]{1,0:T(8,128)S(1)} %collective-permute-done.1, f32[160,128]{1,0:T(8,128)S(1)} %collective-permute-done, f32[160,128]{1,0:T(8,128)} %gain_stage.1), kind=kLoop, calls=%fused_computation.1 | loop fusion | flops 163840 | bytes 655360 | tf_op jit(solution)/shard_map/concatenate | solution.py:337
  43.9 0.1 collective-permute-start.2
  44.0 8.8 %collective-permute-done.2 = f32[640,128]{1,0:T(8,128)S(1)} collective-permute-done((f32[640,128]{1,0:T(8,128)S(1)}, f32[640,128]{1,0:T(8,128)S(1)}, u32[]{:S(2)}, u32[]{:S(2)}) %collective-permute-start.2) | collective-permute-done | bytes 327712 | tf_op jit(solution)/shard_map/ppermute | solution.py:336
  52.8 0.9 %pad_maximum_fusion = f32[1280,128]{1,0:T(8,128)S(1)} fusion(f32[640,128]{1,0:T(8,128)S(1)} %collective-permute-done.2, f32[320,128]{1,0:T(8,128)S(1)} %collective-permute-done.1, f32[160,128]{1,0:T(8,128)S(1)} %collective-permute-done, f32[160,128]{1,0:T(8,128)} %gain_stage.1), kind=kLoop, calls=%fused_computation | loop fusion | flops 491520 | bytes 1310720 | tf_op jit(solution)/shard_map/concatenate | solution.py:337
  53.7 0.1 collective-permute-start.3
  53.8 5.0 %vote_stage.1 = s32[32,700]{1,0:T(8,128)} custom-call(f32[16,8,512]{2,1,0:T(8,128)} %copy-done), custom_call_target="tpu_custom_call" | custom-call | tf_op jit(solution)/shard_map/vote_stage/pallas_call | solution.py:256
  58.8 0.0 copy-done.1
  58.9 0.0 collective-permute-done.3
  59.0 0.0 copy-start.2
  59.0 1.1 %copy-done.2 = f32[2560,128]{1,0:T(8,128)} copy-done((f32[2560,128]{1,0:T(8,128)}, f32[2560,128]{1,0:T(8,128)S(1)}, u32[]{:S(2)}) %copy-start.2) | copy-done | bytes 1310744
  60.1 3.1 %place_stage.1 = f32[32,40,256]{2,1,0:T(8,128)} custom-call(s32[1]{0:T(128)} %bitcast.8.where_ref, f32[2560,128]{1,0:T(8,128)} %copy-done.2), custom_call_target="tpu_custom_call" | custom-call | tf_op jit(solution)/shard_map/place_stage/pallas_call | solution.py:283
  (5 shorter events, 0.1 us)
Async XLA Ops:
  5.7 17.4 %all-to-all-start = ((f32[16,8,512]{2,1,0:T(8,128)}), f32[16,8,512]{2,1,0:T(8,128)S(1)}, u32[]{:S(2)}, u32[]{:S(2)}) async-start(f32[16,8,512]{2,1,0:T(8,128)} %get-tuple-element.9), calls=%async_computation | async-start | bytes 524288 | tf_op jit(solution)/shard_map/all_to_all | solution.py:329
  23.2 0.7 %copy-start = (f32[16,8,512]{2,1,0:T(8,128)}, f32[16,8,512]{2,1,0:T(8,128)S(1)}, u32[]{:S(2)}) copy-start(f32[16,8,512]{2,1,0:T(8,128)S(1)} %all-to-all-done.packet_ref) | copy-start | bytes 786436
  28.8 30.0 %copy-start.1 = (f32[160,128]{1,0:T(8,128)S(1)}, f32[160,128]{1,0:T(8,128)}, u32[]{:S(2)}) copy-start(f32[160,128]{1,0:T(8,128)} %gain_stage.1) | copy-start | bytes 245764
  28.8 7.1 %collective-permute-start = (f32[160,128]{1,0:T(8,128)}, f32[160,128]{1,0:T(8,128)S(1)}, u32[]{:S(2)}, u32[]{:S(2)}) collective-permute-start(f32[160,128]{1,0:T(8,128)} %gain_stage.1), channel_id=1, source_target_pairs={{0,8},{1,9},{2,10},{3,11},{4,12},{5,13},{6,14},{7,15},{8,0},{9,1},... | collective-permute-start | bytes 245768 | tf_op jit(solution)/shard_map/ppermute | solution.py:336
  36.8 6.2 %collective-permute-start.1 = (f32[320,128]{1,0:T(8,128)S(1)}, f32[320,128]{1,0:T(8,128)S(1)}, u32[]{:S(2)}, u32[]{:S(2)}) collective-permute-start(f32[320,128]{1,0:T(8,128)S(1)} %pad_maximum_fusion.2), channel_id=1, source_target_pairs={{0,4},{1,5},{2,6},{3,7},{4,0},{5,1},{6,2},{7,3},{8,12},{9,13},{10,... | collective-permute-start | bytes 491528 | tf_op jit(solution)/shard_map/ppermute | solution.py:336
  43.9 8.8 %collective-permute-start.2 = (f32[640,128]{1,0:T(8,128)S(1)}, f32[640,128]{1,0:T(8,128)S(1)}, u32[]{:S(2)}, u32[]{:S(2)}) collective-permute-start(f32[640,128]{1,0:T(8,128)S(1)} %pad_maximum_fusion.1), channel_id=1, source_target_pairs={{0,2},{1,3},{2,0},{3,1},{4,6},{5,7},{6,4},{7,5},{8,10},{9,11},{10,... | collective-permute-start | bytes 983048 | tf_op jit(solution)/shard_map/ppermute | solution.py:336
  53.7 5.2 %collective-permute-start.3 = (f32[1280,128]{1,0:T(8,128)S(1)}, f32[1280,128]{1,0:T(8,128)S(1)}, u32[]{:S(2)}, u32[]{:S(2)}) collective-permute-start(f32[1280,128]{1,0:T(8,128)S(1)} %pad_maximum_fusion), channel_id=1, source_target_pairs={{0,1},{1,0},{2,3},{3,2},{4,5},{5,4},{6,7},{7,6},{8,9},{9,8},{10,11... | collective-permute-start | bytes 1966088 | tf_op jit(solution)/shard_map/ppermute | solution.py:336
  59.0 1.1 %copy-start.2 = (f32[2560,128]{1,0:T(8,128)}, f32[2560,128]{1,0:T(8,128)S(1)}, u32[]{:S(2)}) copy-start(f32[2560,128]{1,0:T(8,128)S(1)} %constant_dynamic-update-slice_fusion.block_ref) | copy-start | bytes 3932164

commit v2 on v1

v2 whole, which is shorter than its diff:
```python
import jax
import jax.numpy as jnp
from jax import lax
from jax.experimental import pallas as pl
from jax.experimental.pallas import tpu as pltpu
from jax.sharding import PartitionSpec as P

B = 256
LANES = 128
HALVES = B // LANES
LEVELS = 4

ridge_weight = 1.0


def cdiv(a, b):
    return -(-a // b)


def round_up(a, b):
    return cdiv(a, b) * b


def query_rows(score, level, rank, lengths, slots):
    documents = score.shape[1]
    queries = documents // slots
    gain = jnp.left_shift(1, level).astype(jnp.float32) - 1.0
    discount = 1.0 / jnp.log2(rank.astype(jnp.float32) + 2.0)
    place = lax.broadcasted_iota(jnp.int32, (1, slots), 1)
    place_discount = 1.0 / jnp.log2(place.astype(jnp.float32) + 2.0)
    gradients = []
    hessians = []
    for q in range(queries):
        lanes = slice(q * slots, (q + 1) * slots)
        live = place < lengths[q]
        live_row = live.astype(jnp.float32)
        score_row = score[:, lanes]
        gain_row = gain[:, lanes]
        discount_row = discount[:, lanes]
        level_row = jnp.where(live, level[:, lanes], -1)
        ideal_gain = jnp.zeros((1, slots), jnp.float32)
        for v in range(1, LEVELS + 1):
            count = jnp.sum((level_row >= v).astype(jnp.float32), axis=1, keepdims=True)
            ideal_gain = ideal_gain + jnp.where(
                place.astype(jnp.float32) < count, float(2 ** (v - 1)), 0.0
            )
        ideal = jnp.sum(ideal_gain * place_discount, axis=1, keepdims=True)
        scaling = 1.0 / jnp.maximum(ideal, 1.0)
        rows = jnp.concatenate(
            [score_row, gain_row, discount_row, live_row, jnp.zeros((4, slots), jnp.float32)],
            axis=0,
        )
        columns = rows.T
        step = 32
        push_sum = jnp.zeros((8, slots), jnp.float32)
        curve_sum = jnp.zeros((8, slots), jnp.float32)
        for r in range(0, slots, step):
            part = columns[r : r + step]
            gap = (part[:, 1:2] - gain_row) * part[:, 3:4]
            change = gap * jnp.abs(part[:, 2:3] - discount_row)
            lead = score_row - part[:, 0:1]
            chance = 1.0 / (1.0 + jnp.exp(jnp.where(gap > 0.0, -lead, lead)))
            push = chance * change
            curve = (1.0 - chance) * jnp.abs(push)
            for k in range(0, step, 8):
                push_sum = push_sum + push[k : k + 8]
                curve_sum = curve_sum + curve[k : k + 8]
        factor = scaling * live_row
        gradients.append(jnp.sum(push_sum, axis=0, keepdims=True) * factor)
        hessians.append(jnp.sum(curve_sum, axis=0, keepdims=True) * factor)
    return jnp.concatenate(gradients, axis=1), jnp.concatenate(hessians, axis=1)


def vmem_array(shape):
    return pltpu.VMEM(shape, jnp.float32)


def in_vmem(x):
    return pltpu.with_memory_space_constraint(x, pltpu.VMEM)


def in_hbm(x):
    return pltpu.with_memory_space_constraint(x, pltpu.HBM)


def local_stage(bins, leaf, score, level, rank, lengths, votes, elected, plan):
    features, documents = bins.shape
    leaves, picked = elected.shape
    kept = votes.shape[0]
    padded = plan["padded"]
    picks = plan["picks"]
    rows = plan["rows"]
    slots = documents // lengths.shape[0]
    group = 8 if leaves % 8 == 0 else leaves
    per_row = LANES // leaves

    def body(bins_ref, leaf_ref, score_ref, level_ref, rank_ref, length_ref, votes_ref,
             elected_ref, grad_ref, hess_ref, packet_ref, square, chosen_ref):
        square[...] = jnp.zeros(square.shape, jnp.float32)
        square[0:leaves, 0:picked] = elected_ref[...].astype(jnp.float32)
        elected_t = square[...].T
        table = bins_ref[...].astype(jnp.float32).astype(jnp.bfloat16)
        leaf_row = leaf_ref[...]
        feature = lax.broadcasted_iota(jnp.int32, (padded, features), 1).astype(jnp.float32)
        chosen = jnp.zeros((padded, documents), jnp.float32)
        for first in range(0, leaves, group):
            hot = []
            for l in range(first, first + group):
                hot.append((elected_t[0:padded, l : l + 1] == feature).astype(jnp.float32))
            hot = jnp.concatenate(hot, axis=0).astype(jnp.bfloat16)
            found = jnp.dot(hot, table, preferred_element_type=jnp.float32)
            for i in range(group):
                chosen = jnp.where(
                    leaf_row == first + i, found[i * padded : (i + 1) * padded], chosen
                )
        chosen_ref[...] = chosen
        gradient, hessian = query_rows(
            score_ref[...], level_ref[...], rank_ref[...], length_ref, slots
        )
        grad_ref[...] = gradient
        hess_ref[...] = hessian
        tail = []
        for k0 in range(0, kept, per_row):
            line = jnp.zeros((1, LANES), jnp.float32)
            for i in range(min(per_row, kept - k0)):
                values = votes_ref[k0 + i].astype(jnp.float32)
                pieces = [values]
                if i:
                    pieces.insert(0, jnp.zeros((1, i * leaves), jnp.float32))
                if (i + 1) * leaves < LANES:
                    pieces.append(jnp.zeros((1, LANES - (i + 1) * leaves), jnp.float32))
                line = line + jnp.concatenate(pieces, axis=1)
            tail.append(line)
        spare = plan["vote_tiles"] * rows - len(tail)
        if spare:
            tail.append(jnp.zeros((spare, LANES), jnp.float32))
        tail = jnp.concatenate(tail, axis=0)
        shared = [leaf_row.astype(jnp.float32), gradient, hessian]
        if rows > picks + 3:
            shared.append(jnp.zeros((rows - picks - 3, documents), jnp.float32))
        shared = jnp.concatenate(shared, axis=0)
        for j in range(plan["devices"]):
            start = plan["first"][j % plan["owners"]]
            block = jnp.concatenate([chosen_ref[start : start + picks, :], shared], axis=0)
            for c in range(documents // LANES):
                packet_ref[j, c] = block[:, c * LANES : (c + 1) * LANES]
            for t in range(plan["vote_tiles"]):
                packet_ref[j, documents // LANES + t] = tail[t * rows : (t + 1) * rows]

    vmem = pl.BlockSpec(memory_space=pltpu.VMEM)
    return pl.pallas_call(
        body,
        in_specs=[vmem] * 5 + [pl.BlockSpec(memory_space=pltpu.SMEM)] + [vmem] * 2,
        out_specs=[vmem] * 3,
        out_shape=[
            jax.ShapeDtypeStruct((1, documents), jnp.float32),
            jax.ShapeDtypeStruct((1, documents), jnp.float32),
            vmem_array(
                (plan["devices"], documents // LANES + plan["vote_tiles"], rows, LANES)
            ),
        ],
        scratch_shapes=[
            pltpu.VMEM((LANES, LANES), jnp.float32),
            pltpu.VMEM((padded, documents), jnp.float32),
        ],
        compiler_params=pltpu.CompilerParams(vmem_limit_bytes=48 << 20),
        name="local_stage",
    )(*[in_hbm(x) for x in (bins, leaf, score, level, rank, lengths, votes, elected)])


def gain_stage(packets, where, leaves, plan):
    devices = packets.shape[0]
    picks = plan["picks"]
    units = plan["units"]
    chunks = plan["chunks"]
    chunk = 4 if devices % 4 == 0 else 1
    even = units % HALVES == 0

    def body(where_ref, packet_ref, out_ref):
        leaf_id = lax.broadcasted_iota(jnp.int32, (leaves, LANES), 0).astype(jnp.float32)
        bin_id = lax.broadcasted_iota(jnp.int32, (LANES, LANES), 0).astype(jnp.float32)
        local = []
        limit = []
        base = where_ref[0] % plan["owners"] * units
        first = jnp.minimum(base // HALVES, plan["padded"] - picks)
        for i in range(units):
            if even:
                local.append(i // HALVES)
                limit.append(bin_id + float(i % HALVES * LANES))
            else:
                local.append(jnp.clip((base + i) // HALVES - first, 0, picks - 1))
                limit.append(bin_id + ((base + i) % HALVES * LANES).astype(jnp.float32))
        total = jnp.zeros((4 * leaves, units * LANES), jnp.float32)
        grad_all = jnp.zeros((leaves, LANES), jnp.float32)
        hess_all = jnp.zeros((leaves, LANES), jnp.float32)
        for s0 in range(0, devices, chunk):
            weights = []
            steps = [[] for _ in range(units)]
            for s in range(s0, s0 + chunk):
                for c in range(chunks):
                    mine = packet_ref[s, c, picks : picks + 1, :] == leaf_id
                    grad = jnp.where(mine, packet_ref[s, c, picks + 1 : picks + 2, :], 0.0)
                    hess = jnp.where(mine, packet_ref[s, c, picks + 2 : picks + 3, :], 0.0)
                    grad_all = grad_all + grad
                    hess_all = hess_all + hess
                    grad_high = grad.astype(jnp.bfloat16)
                    hess_high = hess.astype(jnp.bfloat16)
                    grad_low = (grad - grad_high.astype(jnp.float32)).astype(jnp.bfloat16)
                    hess_low = (hess - hess_high.astype(jnp.float32)).astype(jnp.bfloat16)
                    weights.append(
                        jnp.concatenate([grad_high, hess_high, grad_low, hess_low], axis=0)
                    )
                    for i in range(units):
                        value = packet_ref[s, c, pl.ds(local[i], 1), :]
                        steps[i].append(
                            (value <= limit[i]).astype(jnp.float32).astype(jnp.bfloat16)
                        )
            weight = jnp.concatenate(weights, axis=1)
            step = jnp.concatenate([jnp.concatenate(p, axis=1) for p in steps], axis=0)
            total = total + lax.dot_general(
                weight, step, (((1,), (1,)), ((), ())), preferred_element_type=jnp.float32
            )
        prefix_grad = total[0:leaves] + total[2 * leaves : 3 * leaves]
        prefix_hess = total[leaves : 2 * leaves] + total[3 * leaves :]
        whole_grad = jnp.sum(grad_all, axis=1, keepdims=True)
        whole_hess = jnp.sum(hess_all, axis=1, keepdims=True)
        rest_grad = whole_grad - prefix_grad
        rest_hess = whole_hess - prefix_hess
        gains = (
            prefix_grad * prefix_grad / (prefix_hess + ridge_weight)
            + rest_grad * rest_grad / (rest_hess + ridge_weight)
            - whole_grad * whole_grad / (whole_hess + ridge_weight)
        )
        for i in range(units):
            out_ref[i * leaves : (i + 1) * leaves, :] = gains[:, i * LANES : (i + 1) * LANES]

    vmem = pl.BlockSpec(memory_space=pltpu.VMEM)
    return pl.pallas_call(
        body,
        in_specs=[pl.BlockSpec(memory_space=pltpu.SMEM), vmem],
        out_specs=vmem,
        out_shape=vmem_array((units * leaves, LANES)),
        compiler_params=pltpu.CompilerParams(vmem_limit_bytes=48 << 20),
        name="gain_stage",
    )(where, in_vmem(packets))


def vote_stage(packets, features, leaves, kept, plan):
    devices = packets.shape[0]
    rows = plan["rows"]
    lines = cdiv(kept * leaves, LANES)
    padded = round_up(features, 8)
    step = 64
    depth = round_up(padded, LANES)

    def body(packet_ref, out_ref, count):
        lane = lax.broadcasted_iota(jnp.int32, (1, LANES), 1)

        def block(index, carry):
            start = pl.multiple_of(index * step, step)
            feature = (lax.broadcasted_iota(jnp.int32, (step, LANES), 0) + start).astype(
                jnp.float32
            )
            total = jnp.zeros((step, LANES), jnp.float32)
            for s in range(devices):
                for line in range(lines):
                    row = line % rows
                    values = packet_ref[s, plan["chunks"] + line // rows, row : row + 1, :]
                    inside = kept * leaves - line * LANES
                    if inside < LANES:
                        values = jnp.where(lane < inside, values, -1.0)
                    total = total + (values == feature).astype(jnp.float32)
            count[pl.ds(start, step), :] = total
            return carry

        lax.fori_loop(0, depth // step, block, 0)
        turned = count[...].T
        summed = turned[0:leaves]
        for i in range(1, LANES // leaves):
            summed = summed + turned[i * leaves : (i + 1) * leaves]
        out_ref[...] = summed[:, 0:features].astype(jnp.int32)

    vmem = pl.BlockSpec(memory_space=pltpu.VMEM)
    return pl.pallas_call(
        body,
        in_specs=[vmem],
        out_specs=vmem,
        out_shape=jax.ShapeDtypeStruct((leaves, features), jnp.int32),
        scratch_shapes=[pltpu.VMEM((depth, LANES), jnp.float32)],
        compiler_params=pltpu.CompilerParams(vmem_limit_bytes=48 << 20),
        cost_estimate=pl.CostEstimate(flops=40_000_000, bytes_accessed=400_000, transcendentals=0),
        name="vote_stage",
    )(in_vmem(packets))


def place_stage(blocks, where, leaves, picked, plan):
    units = plan["units"]
    owners = plan["owners"]
    step = 8 if leaves % 8 == 0 else leaves

    def body(where_ref, *refs):
        out_ref = refs[-1]
        here = where_ref[0] % owners
        first = pl.program_id(0) * step
        odd = here & 1
        for index, ref in enumerate(refs[:-1]):
            owner = index
            if plan["doubling"]:
                near, far = plan["tags"][index % len(plan["tags"])]
                if index < len(plan["tags"]):
                    owner = here ^ jnp.where(odd == 1, far, near)
                else:
                    owner = here ^ 1 ^ jnp.where(odd == 1, near, far)

            def write(target, ref=ref):
                for i in range(units):
                    unit = target * units + i
                    if unit < picked * HALVES:
                        start = pl.multiple_of(i * leaves + first, step)
                        lane = unit % HALVES * LANES
                        out_ref[:, unit // HALVES, lane : lane + LANES] = ref[
                            pl.ds(start, step), :
                        ]

            if plan["doubling"]:
                for target in range(owners):
                    pl.when(owner == target)(lambda target=target, write=write: write(target))
            else:
                write(owner)

    vmem = pl.BlockSpec(memory_space=pltpu.VMEM)
    return pl.pallas_call(
        body,
        grid=(leaves // step,),
        in_specs=[pl.BlockSpec(memory_space=pltpu.SMEM)] + [vmem] * len(blocks),
        out_specs=pl.BlockSpec((step, picked, B), lambda i: (i, 0, 0)),
        out_shape=jax.ShapeDtypeStruct((leaves, picked, B), jnp.float32),
        compiler_params=pltpu.CompilerParams(vmem_limit_bytes=48 << 20),
        name="place_stage",
    )(where, *[in_vmem(b) for b in blocks])


def solution(mesh):
    devices = mesh.shape["rows"]

    def on_device(
        feature_bin, doc_leaf, current_score, relevance, doc_rank, query_length, feature_votes,
        elected,
    ):
        documents, features = feature_bin.shape
        leaves, picked = elected.shape
        kept = feature_votes.shape[2]
        doubling = devices >= 8 and devices & (devices - 1) == 0
        owners = devices // 2 if doubling else devices
        units = cdiv(picked * HALVES, owners)
        padded = round_up(picked, 8)
        picks = max(
            (j * units + units - 1) // HALVES - (j * units) // HALVES + 1 for j in range(owners)
        )
        rows = round_up(picks + 3, 8)
        plan = {
            "devices": devices,
            "doubling": doubling,
            "owners": owners,
            "units": units,
            "picks": picks,
            "padded": padded,
            "first": [min(j * units // HALVES, padded - picks) for j in range(owners)],
            "rows": rows,
            "chunks": documents // LANES,
            "vote_tiles": cdiv(cdiv(kept * leaves, LANES), rows),
        }
        where = lax.axis_index("rows").astype(jnp.int32).reshape(1)
        gradient, hessian, packets = local_stage(
            feature_bin.T,
            doc_leaf.reshape(1, -1),
            current_score.reshape(1, -1),
            relevance.reshape(1, -1),
            doc_rank.reshape(1, -1),
            query_length,
            feature_votes.transpose(2, 0, 1),
            elected,
            plan,
        )
        received = lax.all_to_all(packets, "rows", 0, 0)
        block = gain_stage(received, where, leaves, plan)
        vote_count = vote_stage(received, features, leaves, kept, plan)
        if doubling:
            far = [1 << b for b in reversed(range(1, owners.bit_length() - 1))]
            twin = list(far)
            twin[-2:] = twin[-2:][::-1]
            pairs = [
                [(i, i ^ (twin[p] if i & 1 else far[p])) for i in range(devices)]
                for p in range(len(far))
            ]
            blocks = [block]
            tags = [(0, 0)]
            for p in range(len(far)):
                moved = [lax.ppermute(b, "rows", pairs[p]) for b in blocks]
                if p == 0:
                    moved[0], vote_count = lax.optimization_barrier((moved[0], vote_count))
                blocks = blocks + moved
                tags = tags + [(even | far[p], odd | twin[p]) for even, odd in tags]
            sibling = [(i, i ^ 1) for i in range(devices)]
            blocks = blocks + [lax.ppermute(b, "rows", sibling) for b in blocks]
            plan["tags"] = tags
        else:
            gathered = lax.all_gather(block, "rows", axis=0)
            blocks = [gathered[j] for j in range(devices)]
            plan["tags"] = None
        split_gain = place_stage(blocks, where, leaves, picked, plan)
        return gradient.reshape(-1), hessian.reshape(-1), vote_count, split_gain

    return jax.shard_map(
        on_device,
        mesh=mesh,
        in_specs=(
            P(("parts", "rows"), None),
            P(("parts", "rows")),
            P(("parts", "rows")),
            P(("parts", "rows")),
            P(("parts", "rows")),
            P(("parts", "rows")),
            P(("parts", "rows"), None, None),
            P("parts", None),
        ),
        out_specs=(
            P(("parts", "rows")),
            P(("parts", "rows")),
            P("parts", None),
            P("parts", None, None),
        ),
        check_vma=False,
    )
```

time: 63.7 us -> 46.5 us (0.73)
  waiting for transfers between devices: 30.9 us -> 18.1 us
  local copies, waits for them, and re-layouts: 3.26 us -> 0 us
  other arithmetic: 2.74 us -> 0 us
  Pallas kernels: 16.9 us -> 18.1 us
  starting transfers between devices: 8.69 us -> 9.4 us
    ppermute x4 -> x7, waiting for transfers between devices: 20.9 us -> 7.01 us  [the longest x3 5.63 us: on_device(): moved = [lax.ppermute(b, 'rows', pairs[p]) for b in blocks]]
    unnamed x11 -> x0, local copies, waits for them, and re-layouts: 3.22 us -> none
    concatenate x3 -> x0, other arithmetic: 2.74 us -> none  [on_device(): gathered = jnp.concatenate([gathered, other], axis=0)]
    pallas_call x1, Pallas kernels: 4.97 us -> 7 us  [gain_stage(): pl.pallas_call(body, in_specs=[pl.BlockSpec(memory_space=pltpu.SMEM), vme...]
    all_to_all x1, waiting for transfers between devices: 10 us -> 11.1 us  [on_device(): received = lax.all_to_all(packets, 'rows', 0, 0)]
    ppermute x4 -> x7, starting transfers between devices: 1.27 us -> 1.99 us  [the longest x3 1.47 us: on_device(): moved = [lax.ppermute(b, 'rows', pairs[p]) for b in blocks]]
    pallas_call x1, Pallas kernels: 5.05 us -> 4.39 us  [vote_stage(): pl.pallas_call(body, in_specs=[vmem], out_specs=vmem, out_shape=jax.Shape...]
  transfers between devices with their start and end apart: 5 -> 8, of which waited for: 4 -> 4; matrix products, arithmetic and copies ran while one was open for 0% -> 0% of each run, Pallas kernels for 8% -> 9%
where the time goes in v2:
time: 46.5 us; the launch traced here: 46.2 us
  Pallas kernels  18.1 us (39%)
  waiting for transfers between devices  18.1 us (39%)
  starting transfers between devices  9.4 us (20%)
  between operations  0.67 us (1%)
    all_to_all x1, waiting for transfers between devices, on_device(): received = lax.all_to_all(packets, 'rows', 0, 0)  11.1 us
    all_to_all x1, starting transfers between devices, on_device(): received = lax.all_to_all(packets, 'rows', 0, 0)  7.41 us
    pallas_call x1, Pallas kernels, gain_stage(): pl.pallas_call(body, in_specs=[pl.BlockSpec(memory_space=pltpu.SMEM), vme...  7 us
    ppermute x3, waiting for transfers between devices, on_device(): moved = [lax.ppermute(b, 'rows', pairs[p]) for b in blocks]  5.63 us
    pallas_call x1, Pallas kernels, vote_stage(): pl.pallas_call(body, in_specs=[vmem], out_specs=vmem, out_shape=jax.Shape...  4.39 us
    pallas_call x1, Pallas kernels, local_stage(): pl.pallas_call(body, in_specs=[vmem] * 5 + [pl.BlockSpec(memory_space=plt...  3.64 us
    pallas_call x1, Pallas kernels, place_stage(): pl.pallas_call(body, grid=(leaves // step,), in_specs=[pl.BlockSpec(memor...  3.05 us
    ppermute x3, starting transfers between devices, on_device(): moved = [lax.ppermute(b, 'rows', pairs[p]) for b in blocks]  1.47 us
  transfers between devices with their start and end apart: 8, of which 4 were waited for; matrix products, arithmetic and copies ran while one was open for 0% of the time, Pallas kernels for 9%

profile of v2, /device:TPU:0, one launch (start us, length us, event | category | flops | bytes accessed | tf_op | source)
XLA Modules:
  0.0 46.2 jit_solution(17114781615022837470)
XLA Ops:
  0.6 3.6 %local_stage.1 = (f32[1,512]{1,0:T(1,128)}, f32[1,512]{1,0:T(1,128)}, f32[16,5,8,128]{3,2,1,0:T(8,128)}) custom-call(s32[700,512]{1,0:T(8,128)} %bitcast.9, s32[1,512]{1,0:T(1,128)} %bitcast.11, f32[1,512]{1,0:T(1,128)} %bitcast.12, s32[1,512]{1,0:T(1,128)} %bitcast.13, s32[1,512]{1,0:T(1,128)} %bitcast.14, s32[2]{0:T(128)} %length_ref.1, ...), custom_call_target="tpu_custom_call" | custom-call | tf_op jit(solution)/shard_map/local_stage/pallas_call | solution.py:151
  4.3 7.4 %all-to-all-start = ((f32[16,5,8,128]{3,2,1,0:T(8,128)}), f32[16,5,8,128]{3,2,1,0:T(8,128)S(1)}, u32[]{:S(2)}, u32[]{:S(2)}) async-start(f32[16,5,8,128]{3,2,1,0:T(8,128)} %get-tuple-element.11), calls=%async_computation | async-start | bytes 655360 | tf_op jit(solution)/shard_map/all_to_all | solution.py:385
  11.7 11.1 %all-to-all-done.packet_ref = f32[16,5,8,128]{3,2,1,0:T(8,128)S(1)} async-done(((f32[16,5,8,128]{3,2,1,0:T(8,128)}), f32[16,5,8,128]{3,2,1,0:T(8,128)S(1)}, u32[]{:S(2)}, u32[]{:S(2)}) %all-to-all-start) | async-done | bytes 327712 | tf_op jit(solution)/shard_map/all_to_all | solution.py:385
  22.8 7.0 %gain_stage.1.refs_0_ = f32[320,128]{1,0:T(8,128)S(1)} custom-call(s32[1]{0:T(128)} %bitcast.8.where_ref, f32[16,5,8,128]{3,2,1,0:T(8,128)S(1)} %all-to-all-done.packet_ref), custom_call_target="tpu_custom_call" | custom-call | tf_op jit(solution)/shard_map/gain_stage/pallas_call | solution.py:238
  29.8 0.2 collective-permute-start
  30.0 1.2 %collective-permute-start.1 = (f32[320,128]{1,0:T(8,128)S(1)}, f32[320,128]{1,0:T(8,128)S(1)}, u32[]{:S(2)}, u32[]{:S(2)}) collective-permute-start(f32[320,128]{1,0:T(8,128)S(1)} %gain_stage.1.refs_0_), channel_id=1, source_target_pairs={{0,2},{1,5},{2,0},{3,7},{4,6},{5,1},{6,4},{7,3},{8,10},{9,13},{10,... | collective-permute-start | bytes 491528 | tf_op jit(solution)/shard_map/ppermute | solution.py:399
  31.2 4.4 %vote_stage.1 = s32[32,700]{1,0:T(8,128)} custom-call(f32[16,5,8,128]{3,2,1,0:T(8,128)S(1)} %all-to-all-done.packet_ref), custom_call_target="tpu_custom_call" | custom-call | flops 40000000 | bytes 400000 | tf_op jit(solution)/shard_map/vote_stage/pallas_call | solution.py:284
  35.6 0.8 %collective-permute-done.refs_1_ = f32[320,128]{1,0:T(8,128)S(1)} collective-permute-done((f32[320,128]{1,0:T(8,128)S(1)}, f32[320,128]{1,0:T(8,128)S(1)}, u32[]{:S(2)}, u32[]{:S(2)}) %collective-permute-start) | collective-permute-done | bytes 163872 | tf_op jit(solution)/shard_map/ppermute | solution.py:399
  36.5 0.0 collective-permute-start.2
  36.5 0.0 collective-permute-start.3
  36.5 0.5 %collective-permute-start.4 = (f32[320,128]{1,0:T(8,128)S(1)}, f32[320,128]{1,0:T(8,128)S(1)}, u32[]{:S(2)}, u32[]{:S(2)}) collective-permute-start(f32[320,128]{1,0:T(8,128)S(1)} %collective-permute-done.refs_1_), channel_id=1, source_target_pairs={{0,1},{1,0},{2,3},{3,2},{4,5},{5,4},{6,7},{7,6},{8,9},{9,8},{10,11... | collective-permute-start | bytes 491528 | tf_op jit(solution)/shard_map/ppermute | solution.py:405
  37.0 0.0 collective-permute-done.1.refs_2_
  37.0 0.0 collective-permute-start.5
  37.0 4.8 %collective-permute-done.2.refs_3_ = f32[320,128]{1,0:T(8,128)S(1)} collective-permute-done((f32[320,128]{1,0:T(8,128)S(1)}, f32[320,128]{1,0:T(8,128)S(1)}, u32[]{:S(2)}, u32[]{:S(2)}) %collective-permute-start.2) | collective-permute-done | bytes 163872 | tf_op jit(solution)/shard_map/ppermute | solution.py:399
  41.8 0.0 collective-permute-start.6
  41.8 0.0 collective-permute-done.3.refs_4_
  41.8 0.0 collective-permute-done.5.refs_6_
  41.8 0.0 collective-permute-done.4.refs_5_
  41.8 1.4 %collective-permute-done.6.refs_7_ = f32[320,128]{1,0:T(8,128)S(1)} collective-permute-done((f32[320,128]{1,0:T(8,128)S(1)}, f32[320,128]{1,0:T(8,128)S(1)}, u32[]{:S(2)}, u32[]{:S(2)}) %collective-permute-start.6) | collective-permute-done | bytes 163872 | tf_op jit(solution)/shard_map/ppermute | solution.py:405
  43.2 3.0 %place_stage.1 = f32[32,40,256]{2,1,0:T(8,128)} custom-call(s32[1]{0:T(128)} %bitcast.8.where_ref, f32[320,128]{1,0:T(8,128)S(1)} %gain_stage.1.refs_0_, f32[320,128]{1,0:T(8,128)S(1)} %collective-permute-done.refs_1_, f32[320,128]{1,0:T(8,128)S(1)} %collective-permute-done.1.refs_2_, f32[320,128]{1,0:T(8,128)S(1)} %collective-permute-done.2.refs_3_, ...), custom_call_target="tpu_custom_call" | custom-call | tf_op jit(solution)/shard_map/place_stage/pallas_call | solution.py:332
Async XLA Ops:
  4.3 18.5 %all-to-all-start = ((f32[16,5,8,128]{3,2,1,0:T(8,128)}), f32[16,5,8,128]{3,2,1,0:T(8,128)S(1)}, u32[]{:S(2)}, u32[]{:S(2)}) async-start(f32[16,5,8,128]{3,2,1,0:T(8,128)} %get-tuple-element.11), calls=%async_computation | async-start | bytes 655360 | tf_op jit(solution)/shard_map/all_to_all | solution.py:385
  29.8 6.7 %collective-permute-start = (f32[320,128]{1,0:T(8,128)S(1)}, f32[320,128]{1,0:T(8,128)S(1)}, u32[]{:S(2)}, u32[]{:S(2)}) collective-permute-start(f32[320,128]{1,0:T(8,128)S(1)} %gain_stage.1.refs_0_), channel_id=1, source_target_pairs={{0,4},{1,3},{2,6},{3,1},{4,0},{5,7},{6,2},{7,5},{8,12},{9,11},{10,... | collective-permute-start | bytes 491528 | tf_op jit(solution)/shard_map/ppermute | solution.py:399
  30.0 7.0 %collective-permute-start.1 = (f32[320,128]{1,0:T(8,128)S(1)}, f32[320,128]{1,0:T(8,128)S(1)}, u32[]{:S(2)}, u32[]{:S(2)}) collective-permute-start(f32[320,128]{1,0:T(8,128)S(1)} %gain_stage.1.refs_0_), channel_id=1, source_target_pairs={{0,2},{1,5},{2,0},{3,7},{4,6},{5,1},{6,4},{7,3},{8,10},{9,13},{10,... | collective-permute-start | bytes 491528 | tf_op jit(solution)/shard_map/ppermute | solution.py:399
  36.5 5.3 %collective-permute-start.2 = (f32[320,128]{1,0:T(8,128)S(1)}, f32[320,128]{1,0:T(8,128)S(1)}, u32[]{:S(2)}, u32[]{:S(2)}) collective-permute-start(f32[320,128]{1,0:T(8,128)S(1)} %collective-permute-done.refs_1_), channel_id=1, source_target_pairs={{0,2},{1,5},{2,0},{3,7},{4,6},{5,1},{6,4},{7,3},{8,10},{9,13},{10,... | collective-permute-start | bytes 491528 | tf_op jit(solution)/shard_map/ppermute | solution.py:399
  36.5 5.3 %collective-permute-start.3 = (f32[320,128]{1,0:T(8,128)S(1)}, f32[320,128]{1,0:T(8,128)S(1)}, u32[]{:S(2)}, u32[]{:S(2)}) collective-permute-start(f32[320,128]{1,0:T(8,128)S(1)} %gain_stage.1.refs_0_), channel_id=1, source_target_pairs={{0,1},{1,0},{2,3},{3,2},{4,5},{5,4},{6,7},{7,6},{8,9},{9,8},{10,11... | collective-permute-start | bytes 491528 | tf_op jit(solution)/shard_map/ppermute | solution.py:405
  36.5 5.3 %collective-permute-start.4 = (f32[320,128]{1,0:T(8,128)S(1)}, f32[320,128]{1,0:T(8,128)S(1)}, u32[]{:S(2)}, u32[]{:S(2)}) collective-permute-start(f32[320,128]{1,0:T(8,128)S(1)} %collective-permute-done.refs_1_), channel_id=1, source_target_pairs={{0,1},{1,0},{2,3},{3,2},{4,5},{5,4},{6,7},{7,6},{8,9},{9,8},{10,11... | collective-permute-start | bytes 491528 | tf_op jit(solution)/shard_map/ppermute | solution.py:405
  37.0 4.8 %collective-permute-start.5 = (f32[320,128]{1,0:T(8,128)S(1)}, f32[320,128]{1,0:T(8,128)S(1)}, u32[]{:S(2)}, u32[]{:S(2)}) collective-permute-start(f32[320,128]{1,0:T(8,128)S(1)} %collective-permute-done.1.refs_2_), channel_id=1, source_target_pairs={{0,1},{1,0},{2,3},{3,2},{4,5},{5,4},{6,7},{7,6},{8,9},{9,8},{10,11... | collective-permute-start | bytes 491528 | tf_op jit(solution)/shard_map/ppermute | solution.py:405
  41.8 1.4 %collective-permute-start.6 = (f32[320,128]{1,0:T(8,128)S(1)}, f32[320,128]{1,0:T(8,128)S(1)}, u32[]{:S(2)}, u32[]{:S(2)}) collective-permute-start(f32[320,128]{1,0:T(8,128)S(1)} %collective-permute-done.2.refs_3_), channel_id=1, source_target_pairs={{0,1},{1,0},{2,3},{3,2},{4,5},{5,4},{6,7},{7,6},{8,9},{9,8},{10,11... | collective-permute-start | bytes 491528 | tf_op jit(solution)/shard_map/ppermute | solution.py:405

commit v3 on v2

--- a/solution.py
+++ b/solution.py
@@ -95,12 +95,37 @@
     per_row = LANES // leaves
 
     def body(bins_ref, leaf_ref, score_ref, level_ref, rank_ref, length_ref, votes_ref,
-             elected_ref, grad_ref, hess_ref, packet_ref, square, chosen_ref):
+             elected_ref, grad_ref, hess_ref, packet_ref, square, chosen_ref, bins_here, arrived):
+        fetch = pltpu.make_async_copy(bins_ref, bins_here, arrived)
+        fetch.start()
         square[...] = jnp.zeros(square.shape, jnp.float32)
         square[0:leaves, 0:picked] = elected_ref[...].astype(jnp.float32)
         elected_t = square[...].T
-        table = bins_ref[...].astype(jnp.float32).astype(jnp.bfloat16)
         leaf_row = leaf_ref[...]
+        gradient, hessian = query_rows(
+            score_ref[...], level_ref[...], rank_ref[...], length_ref, slots
+        )
+        grad_ref[...] = gradient
+        hess_ref[...] = hessian
+        lane = lax.broadcasted_iota(jnp.int32, (1, documents), 1)
+        starts = [0]
+        for q in range(documents // slots):
+            starts.append(starts[-1] + length_ref[q])
+
+        def compact(block):
+            result = block
+            for q in range(1, documents // slots):
+                moved = pltpu.roll(block, starts[q] - q * slots + documents, 1)
+                result = jnp.where(lane >= starts[q], moved, result)
+            return result
+
+        shared = [leaf_row.astype(jnp.float32), gradient, hessian]
+        shared.append(jnp.zeros((max(rows - picks, 8) - 3, documents), jnp.float32))
+        shared = compact(jnp.concatenate(shared, axis=0))[0 : rows - picks]
+        shared = jnp.where(lane < starts[-1], shared, 0.0)
+        count = jnp.zeros((1, LANES), jnp.float32) + starts[-1].astype(jnp.float32)
+        fetch.wait()
+        table = bins_here[...].astype(jnp.float32).astype(jnp.bfloat16)
         feature = lax.broadcasted_iota(jnp.int32, (padded, features), 1).astype(jnp.float32)
         chosen = jnp.zeros((padded, documents), jnp.float32)
         for first in range(0, leaves, group):
@@ -113,12 +138,7 @@
                 chosen = jnp.where(
                     leaf_row == first + i, found[i * padded : (i + 1) * padded], chosen
                 )
-        chosen_ref[...] = chosen
-        gradient, hessian = query_rows(
-            score_ref[...], level_ref[...], rank_ref[...], length_ref, slots
-        )
-        grad_ref[...] = gradient
-        hess_ref[...] = hessian
+        chosen_ref[...] = compact(chosen)
         tail = []
         for k0 in range(0, kept, per_row):
             line = jnp.zeros((1, LANES), jnp.float32)
@@ -131,14 +151,11 @@
                     pieces.append(jnp.zeros((1, LANES - (i + 1) * leaves), jnp.float32))
                 line = line + jnp.concatenate(pieces, axis=1)
             tail.append(line)
+        tail.append(count)
         spare = plan["vote_tiles"] * rows - len(tail)
         if spare:
             tail.append(jnp.zeros((spare, LANES), jnp.float32))
         tail = jnp.concatenate(tail, axis=0)
-        shared = [leaf_row.astype(jnp.float32), gradient, hessian]
-        if rows > picks + 3:
-            shared.append(jnp.zeros((rows - picks - 3, documents), jnp.float32))
-        shared = jnp.concatenate(shared, axis=0)
         for j in range(plan["devices"]):
             start = plan["first"][j % plan["owners"]]
             block = jnp.concatenate([chosen_ref[start : start + picks, :], shared], axis=0)
@@ -150,7 +167,10 @@
     vmem = pl.BlockSpec(memory_space=pltpu.VMEM)
     return pl.pallas_call(
         body,
-        in_specs=[vmem] * 5 + [pl.BlockSpec(memory_space=pltpu.SMEM)] + [vmem] * 2,
+        in_specs=[pl.BlockSpec(memory_space=pltpu.HBM)]
+        + [vmem] * 4
+        + [pl.BlockSpec(memory_space=pltpu.SMEM)]
+        + [vmem] * 2,
         out_specs=[vmem] * 3,
         out_shape=[
             jax.ShapeDtypeStruct((1, documents), jnp.float32),
@@ -162,6 +182,8 @@
         scratch_shapes=[
             pltpu.VMEM((LANES, LANES), jnp.float32),
             pltpu.VMEM((padded, documents), jnp.float32),
+            pltpu.VMEM((features, documents), jnp.int32),
+            pltpu.SemaphoreType.DMA,
         ],
         compiler_params=pltpu.CompilerParams(vmem_limit_bytes=48 << 20),
         name="local_stage",
@@ -176,7 +198,9 @@
     chunk = 4 if devices % 4 == 0 else 1
     even = units % HALVES == 0
 
-    def body(where_ref, packet_ref, out_ref):
+    half = cdiv(chunks, 2)
+
+    def body(where_ref, packet_ref, out_ref, total_ref, grad_ref, hess_ref):
         leaf_id = lax.broadcasted_iota(jnp.int32, (leaves, LANES), 0).astype(jnp.float32)
         bin_id = lax.broadcasted_iota(jnp.int32, (LANES, LANES), 0).astype(jnp.float32)
         local = []
@@ -190,19 +214,18 @@
             else:
                 local.append(jnp.clip((base + i) // HALVES - first, 0, picks - 1))
                 limit.append(bin_id + ((base + i) % HALVES * LANES).astype(jnp.float32))
-        total = jnp.zeros((4 * leaves, units * LANES), jnp.float32)
-        grad_all = jnp.zeros((leaves, LANES), jnp.float32)
-        hess_all = jnp.zeros((leaves, LANES), jnp.float32)
-        for s0 in range(0, devices, chunk):
+        def terms(sources, parts):
             weights = []
             steps = [[] for _ in range(units)]
-            for s in range(s0, s0 + chunk):
-                for c in range(chunks):
+            grad_sum = jnp.zeros((leaves, LANES), jnp.float32)
+            hess_sum = jnp.zeros((leaves, LANES), jnp.float32)
+            for s in sources:
+                for c in parts:
                     mine = packet_ref[s, c, picks : picks + 1, :] == leaf_id
                     grad = jnp.where(mine, packet_ref[s, c, picks + 1 : picks + 2, :], 0.0)
                     hess = jnp.where(mine, packet_ref[s, c, picks + 2 : picks + 3, :], 0.0)
-                    grad_all = grad_all + grad
-                    hess_all = hess_all + hess
+                    grad_sum = grad_sum + grad
+                    hess_sum = hess_sum + hess
                     grad_high = grad.astype(jnp.bfloat16)
                     hess_high = hess.astype(jnp.bfloat16)
                     grad_low = (grad - grad_high.astype(jnp.float32)).astype(jnp.bfloat16)
@@ -217,9 +240,47 @@
                         )
             weight = jnp.concatenate(weights, axis=1)
             step = jnp.concatenate([jnp.concatenate(p, axis=1) for p in steps], axis=0)
-            total = total + lax.dot_general(
+            product = lax.dot_general(
                 weight, step, (((1,), (1,)), ((), ())), preferred_element_type=jnp.float32
             )
+            return product, grad_sum, hess_sum
+
+        flags = []
+        for s0 in range(0, devices, 16):
+            flag = jnp.zeros((1, LANES), jnp.float32)
+            for s in range(s0, min(s0 + 16, devices)):
+                row = plan["vote_lines"]
+                count = packet_ref[s, chunks + row // plan["rows"], row % plan["rows"], :]
+                flag = flag + jnp.where(
+                    count.reshape(1, LANES) > float(half * LANES), float(1 << (s - s0)), 0.0
+                )
+            flags.append(jnp.max(flag).astype(jnp.int32))
+        total, grad_all, hess_all = terms(range(chunk), range(half))
+        for s0 in range(chunk, devices, chunk):
+            more, grad_more, hess_more = terms(range(s0, s0 + chunk), range(half))
+            total = total + more
+            grad_all = grad_all + grad_more
+            hess_all = hess_all + hess_more
+        total_ref[...] = total
+        grad_ref[...] = grad_all
+        hess_ref[...] = hess_all
+        for s0 in range(0, devices, 16):
+            flag = flags[s0 // 16]
+
+            def late(k, carry, s0=s0, flag=flag):
+                @pl.when((jnp.right_shift(flag, k) & 1) == 1)
+                def _():
+                    more, grad_more, hess_more = terms([s0 + k], range(half, chunks))
+                    total_ref[...] += more
+                    grad_ref[...] += grad_more
+                    hess_ref[...] += hess_more
+
+                return carry
+
+            lax.fori_loop(0, min(16, devices - s0), late, 0)
+        total = total_ref[...]
+        grad_all = grad_ref[...]
+        hess_all = hess_ref[...]
         prefix_grad = total[0:leaves] + total[2 * leaves : 3 * leaves]
         prefix_hess = total[leaves : 2 * leaves] + total[3 * leaves :]
         whole_grad = jnp.sum(grad_all, axis=1, keepdims=True)
@@ -240,20 +301,25 @@
         in_specs=[pl.BlockSpec(memory_space=pltpu.SMEM), vmem],
         out_specs=vmem,
         out_shape=vmem_array((units * leaves, LANES)),
+        scratch_shapes=[
+            pltpu.VMEM((4 * leaves, units * LANES), jnp.float32),
+            pltpu.VMEM((leaves, LANES), jnp.float32),
+            pltpu.VMEM((leaves, LANES), jnp.float32),
+        ],
         compiler_params=pltpu.CompilerParams(vmem_limit_bytes=48 << 20),
         name="gain_stage",
     )(where, in_vmem(packets))
 
 
-def vote_stage(packets, features, leaves, kept, plan):
-    devices = packets.shape[0]
+def vote_stage(packets, before, sources, features, leaves, kept, plan):
     rows = plan["rows"]
-    lines = cdiv(kept * leaves, LANES)
-    padded = round_up(features, 8)
+    lines = plan["vote_lines"]
     step = 64
-    depth = round_up(padded, LANES)
-
-    def body(packet_ref, out_ref, count):
+    depth = round_up(features, LANES)
+    last = before is not None
+
+    def body(packet_ref, *refs):
+        out_ref, count = refs[-2:] if last else (None, refs[-1])
         lane = lax.broadcasted_iota(jnp.int32, (1, LANES), 1)
 
         def block(index, carry):
@@ -262,7 +328,9 @@
                 jnp.float32
             )
             total = jnp.zeros((step, LANES), jnp.float32)
-            for s in range(devices):
+            if last:
+                total = refs[0][pl.ds(start, step), :]
+            for s in sources:
                 for line in range(lines):
                     row = line % rows
                     values = packet_ref[s, plan["chunks"] + line // rows, row : row + 1, :]
@@ -274,23 +342,32 @@
             return carry
 
         lax.fori_loop(0, depth // step, block, 0)
-        turned = count[...].T
-        summed = turned[0:leaves]
-        for i in range(1, LANES // leaves):
-            summed = summed + turned[i * leaves : (i + 1) * leaves]
-        out_ref[...] = summed[:, 0:features].astype(jnp.int32)
+        if last:
+            turned = count[...].T
+            summed = turned[0:leaves]
+            for i in range(1, LANES // leaves):
+                summed = summed + turned[i * leaves : (i + 1) * leaves]
+            out_ref[...] = summed[:, 0:features].astype(jnp.int32)
 
     vmem = pl.BlockSpec(memory_space=pltpu.VMEM)
+    if last:
+        inputs = [in_vmem(packets), in_vmem(before)]
+        out_shape = jax.ShapeDtypeStruct((leaves, features), jnp.int32)
+        scratch = [pltpu.VMEM((depth, LANES), jnp.float32)]
+    else:
+        inputs = [in_vmem(packets)]
+        out_shape = vmem_array((depth, LANES))
+        scratch = []
     return pl.pallas_call(
         body,
-        in_specs=[vmem],
+        in_specs=[vmem] * len(inputs),
         out_specs=vmem,
-        out_shape=jax.ShapeDtypeStruct((leaves, features), jnp.int32),
-        scratch_shapes=[pltpu.VMEM((depth, LANES), jnp.float32)],
+        out_shape=out_shape,
+        scratch_shapes=scratch,
         compiler_params=pltpu.CompilerParams(vmem_limit_bytes=48 << 20),
-        cost_estimate=pl.CostEstimate(flops=40_000_000, bytes_accessed=400_000, transcendentals=0),
+        cost_estimate=pl.CostEstimate(flops=20_000_000, bytes_accessed=400_000, transcendentals=0),
         name="vote_stage",
-    )(in_vmem(packets))
+    )(*inputs)
 
 
 def place_stage(blocks, where, leaves, picked, plan):
@@ -298,46 +375,68 @@
     owners = plan["owners"]
     step = 8 if leaves % 8 == 0 else leaves
 
+    rows = step * picked
+    groups = leaves // step
+
     def body(where_ref, *refs):
-        out_ref = refs[-1]
+        out_ref, planes, done = refs[-3:]
         here = where_ref[0] % owners
-        first = pl.program_id(0) * step
         odd = here & 1
-        for index, ref in enumerate(refs[:-1]):
-            owner = index
-            if plan["doubling"]:
-                near, far = plan["tags"][index % len(plan["tags"])]
-                if index < len(plan["tags"]):
-                    owner = here ^ jnp.where(odd == 1, far, near)
-                else:
-                    owner = here ^ 1 ^ jnp.where(odd == 1, near, far)
-
-            def write(target, ref=ref):
+        owner = []
+        for index in range(len(blocks)):
+            if not plan["doubling"]:
+                owner.append(index)
+                continue
+            even_tag, odd_tag = plan["tags"][index % len(plan["tags"])]
+            if index < len(plan["tags"]):
+                owner.append(here ^ jnp.where(odd == 1, odd_tag, even_tag))
+            else:
+                owner.append(here ^ 1 ^ jnp.where(odd == 1, even_tag, odd_tag))
+        copies = []
+        for g in range(groups):
+            for index, ref in enumerate(refs[:-3]):
                 for i in range(units):
-                    unit = target * units + i
-                    if unit < picked * HALVES:
-                        start = pl.multiple_of(i * leaves + first, step)
-                        lane = unit % HALVES * LANES
-                        out_ref[:, unit // HALVES, lane : lane + LANES] = ref[
-                            pl.ds(start, step), :
+
+                    def write(index=index, ref=ref, i=i):
+                        if units % HALVES == 0:
+                            half = i % HALVES
+                            pick = owner[index] * (units // HALVES) + i // HALVES
+                        else:
+                            half = (owner[index] * units + i) % HALVES
+                            pick = (owner[index] * units + i) // HALVES
+                        start = i * leaves + g * step
+                        planes[half, pl.ds(g * rows + pick, step, stride=picked), :] = ref[
+                            start : start + step, :
                         ]
 
-            if plan["doubling"]:
-                for target in range(owners):
-                    pl.when(owner == target)(lambda target=target, write=write: write(target))
-            else:
-                write(owner)
+                    if owners * units == picked * HALVES:
+                        write()
+                    else:
+                        pl.when(owner[index] * units + i < picked * HALVES)(write)
+            for half in range(HALVES):
+                copy = pltpu.make_async_copy(
+                    planes.at[half, pl.ds(g * rows, rows), :],
+                    out_ref.at[pl.ds(g * rows, rows), pl.ds(half * LANES, LANES)],
+                    done.at[g * HALVES + half],
+                )
+                copy.start()
+                copies.append(copy)
+        for copy in copies:
+            copy.wait()
 
     vmem = pl.BlockSpec(memory_space=pltpu.VMEM)
     return pl.pallas_call(
         body,
-        grid=(leaves // step,),
         in_specs=[pl.BlockSpec(memory_space=pltpu.SMEM)] + [vmem] * len(blocks),
-        out_specs=pl.BlockSpec((step, picked, B), lambda i: (i, 0, 0)),
-        out_shape=jax.ShapeDtypeStruct((leaves, picked, B), jnp.float32),
+        out_specs=pl.BlockSpec(memory_space=pltpu.HBM),
+        out_shape=jax.ShapeDtypeStruct((leaves * picked, B), jnp.float32),
+        scratch_shapes=[
+            pltpu.VMEM((HALVES, leaves * picked, LANES), jnp.float32),
+            pltpu.SemaphoreType.DMA((groups * HALVES,)),
+        ],
         compiler_params=pltpu.CompilerParams(vmem_limit_bytes=48 << 20),
         name="place_stage",
-    )(where, *[in_vmem(b) for b in blocks])
+    )(where, *[in_vmem(b) for b in blocks]).reshape(leaves, picked, B)
 
 
 def solution(mesh):
@@ -368,7 +467,8 @@
             "first": [min(j * units // HALVES, padded - picks) for j in range(owners)],
             "rows": rows,
             "chunks": documents // LANES,
-            "vote_tiles": cdiv(cdiv(kept * leaves, LANES), rows),
+            "vote_lines": cdiv(kept * leaves, LANES),
+            "vote_tiles": cdiv(cdiv(kept * leaves, LANES) + 1, rows),
         }
         where = lax.axis_index("rows").astype(jnp.int32).reshape(1)
         gradient, hessian, packets = local_stage(
@@ -384,7 +484,9 @@
         )
         received = lax.all_to_all(packets, "rows", 0, 0)
         block = gain_stage(received, where, leaves, plan)
-        vote_count = vote_stage(received, features, leaves, kept, plan)
+        middle = cdiv(devices, 2)
+        count_args = (features, leaves, kept, plan)
+        votes = vote_stage(received, None, range(middle), *count_args)
         if doubling:
             far = [1 << b for b in reversed(range(1, owners.bit_length() - 1))]
             twin = list(far)
@@ -397,19 +499,23 @@
             tags = [(0, 0)]
             for p in range(len(far)):
                 moved = [lax.ppermute(b, "rows", pairs[p]) for b in blocks]
-                if p == 0:
-                    moved[0], vote_count = lax.optimization_barrier((moved[0], vote_count))
+                if p == len(far) - 1:
+                    votes = vote_stage(received, votes, range(middle, devices), *count_args)
+                    moved[-1], votes = lax.optimization_barrier((moved[-1], votes))
+                elif p == len(far) - 2:
+                    moved[0], votes = lax.optimization_barrier((moved[0], votes))
                 blocks = blocks + moved
                 tags = tags + [(even | far[p], odd | twin[p]) for even, odd in tags]
             sibling = [(i, i ^ 1) for i in range(devices)]
             blocks = blocks + [lax.ppermute(b, "rows", sibling) for b in blocks]
             plan["tags"] = tags
         else:
+            votes = vote_stage(received, votes, range(middle, devices), *count_args)
             gathered = lax.all_gather(block, "rows", axis=0)
             blocks = [gathered[j] for j in range(devices)]
             plan["tags"] = None
         split_gain = place_stage(blocks, where, leaves, picked, plan)
-        return gradient.reshape(-1), hessian.reshape(-1), vote_count, split_gain
+        return gradient.reshape(-1), hessian.reshape(-1), votes, split_gain
 
     return jax.shard_map(
         on_device,

time: 46.5 us -> 43.2 us (0.929); the launches traced: 46.2 us -> 43.6 us
  Pallas kernels: 18.1 us -> 15.4 us
    pallas_call x3 -> x4, Pallas kernels: 11.1 us -> 9.75 us  [the longest x2 4.33 us: vote_stage(): pl.pallas_call(body, in_specs=[vmem] * len(inputs), out_specs=vmem, out_s...]
    pallas_call x1, Pallas kernels: 7 us -> 5.68 us  [gain_stage(): pl.pallas_call(body, in_specs=[pl.BlockSpec(memory_space=pltpu.SMEM), vme...]
  transfers between devices with their start and end apart: 8 -> 8, of which waited for: 4 -> 4; matrix products, arithmetic and copies ran while one was open for 0% -> 0% of each run, Pallas kernels for 9% -> 10%
where the time goes in v3:
time: 43.2 us; the launch traced here: 43.6 us
  waiting for transfers between devices  18.1 us (42%)
  Pallas kernels  15.4 us (36%)
  starting transfers between devices  9.41 us (22%)
  between operations  0.68 us (2%)
    all_to_all x1, waiting for transfers between devices, on_device(): received = lax.all_to_all(packets, 'rows', 0, 0)  11.1 us
    all_to_all x1, starting transfers between devices, on_device(): received = lax.all_to_all(packets, 'rows', 0, 0)  7.43 us
    ppermute x3, waiting for transfers between devices, on_device(): moved = [lax.ppermute(b, 'rows', pairs[p]) for b in blocks]  5.69 us
    pallas_call x1, Pallas kernels, gain_stage(): pl.pallas_call(body, in_specs=[pl.BlockSpec(memory_space=pltpu.SMEM), vme...  5.68 us
    pallas_call x2, Pallas kernels, vote_stage(): pl.pallas_call(body, in_specs=[vmem] * len(inputs), out_specs=vmem, out_s...  4.33 us
    pallas_call x1, Pallas kernels, local_stage(): pl.pallas_call(body, in_specs=[pl.BlockSpec(memory_space=pltpu.HBM)] + [v...  4.24 us
    ppermute x3, starting transfers between devices, on_device(): moved = [lax.ppermute(b, 'rows', pairs[p]) for b in blocks]  1.46 us
    ppermute x4, waiting for transfers between devices, on_device(): blocks = blocks + [lax.ppermute(b, 'rows', sibling) for b in blocks]  1.38 us
  transfers between devices with their start and end apart: 8, of which 4 were waited for; matrix products, arithmetic and copies ran while one was open for 0% of the time, Pallas kernels for 10%

profile of v3, /device:TPU:0, one launch (start us, length us, event | category | flops | bytes accessed | tf_op | source)
XLA Modules:
  0.0 43.6 jit_solution(8696781263544370736)
XLA Ops:
  0.6 4.2 %local_stage.1 = (f32[1,512]{1,0:T(1,128)}, f32[1,512]{1,0:T(1,128)}, f32[16,5,8,128]{3,2,1,0:T(8,128)}) custom-call(s32[700,512]{1,0:T(8,128)} %bitcast.10, s32[1,512]{1,0:T(1,128)} %bitcast.13, f32[1,512]{1,0:T(1,128)} %bitcast.14, s32[1,512]{1,0:T(1,128)} %bitcast.15, s32[1,512]{1,0:T(1,128)} %bitcast.16, s32[2]{0:T(128)} %length_ref.1, ...), custom_call_target="tpu_custom_call" | custom-call | tf_op jit(solution)/shard_map/local_stage/pallas_call | solution.py:168
  4.9 7.4 %all-to-all-start = ((f32[16,5,8,128]{3,2,1,0:T(8,128)}), f32[16,5,8,128]{3,2,1,0:T(8,128)S(1)}, u32[]{:S(2)}, u32[]{:S(2)}) async-start(f32[16,5,8,128]{3,2,1,0:T(8,128)} %get-tuple-element.13), calls=%async_computation | async-start | bytes 655360 | tf_op jit(solution)/shard_map/all_to_all | solution.py:485
  12.3 11.1 %all-to-all-done.packet_ref = f32[16,5,8,128]{3,2,1,0:T(8,128)S(1)} async-done(((f32[16,5,8,128]{3,2,1,0:T(8,128)}), f32[16,5,8,128]{3,2,1,0:T(8,128)S(1)}, u32[]{:S(2)}, u32[]{:S(2)}) %all-to-all-start) | async-done | bytes 327712 | tf_op jit(solution)/shard_map/all_to_all | solution.py:485
  23.4 5.7 %gain_stage.1.refs_0_ = f32[320,128]{1,0:T(8,128)S(1)} custom-call(s32[1]{0:T(128)} %bitcast.8.where_ref, f32[16,5,8,128]{3,2,1,0:T(8,128)S(1)} %all-to-all-done.packet_ref), custom_call_target="tpu_custom_call" | custom-call | tf_op jit(solution)/shard_map/gain_stage/pallas_call | solution.py:299
  29.1 0.2 collective-permute-start
  29.3 1.2 %collective-permute-start.2 = (f32[320,128]{1,0:T(8,128)S(1)}, f32[320,128]{1,0:T(8,128)S(1)}, u32[]{:S(2)}, u32[]{:S(2)}) collective-permute-start(f32[320,128]{1,0:T(8,128)S(1)} %gain_stage.1.refs_0_), channel_id=1, source_target_pairs={{0,2},{1,5},{2,0},{3,7},{4,6},{5,1},{6,4},{7,3},{8,10},{9,13},{10,... | collective-permute-start | bytes 491528 | tf_op jit(solution)/shard_map/ppermute | solution.py:501
  30.5 1.8 %vote_stage.2.refs_0_ = f32[768,128]{1,0:T(8,128)S(1)} custom-call(f32[16,5,8,128]{3,2,1,0:T(8,128)S(1)} %all-to-all-done.packet_ref), custom_call_target="tpu_custom_call" | custom-call | flops 20000000 | bytes 400000 | tf_op jit(solution)/shard_map/vote_stage/pallas_call | solution.py:361
  32.3 3.4 %collective-permute-done.refs_1_ = f32[320,128]{1,0:T(8,128)S(1)} collective-permute-done((f32[320,128]{1,0:T(8,128)S(1)}, f32[320,128]{1,0:T(8,128)S(1)}, u32[]{:S(2)}, u32[]{:S(2)}) %collective-permute-start) | collective-permute-done | bytes 163872 | tf_op jit(solution)/shard_map/ppermute | solution.py:501
  35.8 0.0 collective-permute-start.1
  35.8 0.0 collective-permute-start.3
  35.8 0.5 %collective-permute-start.4 = (f32[320,128]{1,0:T(8,128)S(1)}, f32[320,128]{1,0:T(8,128)S(1)}, u32[]{:S(2)}, u32[]{:S(2)}) collective-permute-start(f32[320,128]{1,0:T(8,128)S(1)} %collective-permute-done.refs_1_), channel_id=1, source_target_pairs={{0,1},{1,0},{2,3},{3,2},{4,5},{5,4},{6,7},{7,6},{8,9},{9,8},{10,11... | collective-permute-start | bytes 491528 | tf_op jit(solution)/shard_map/ppermute | solution.py:510
  36.3 0.0 collective-permute-done.2.refs_2_
  36.3 0.0 collective-permute-start.5
  36.3 2.5 %vote_stage.3 = s32[32,700]{1,0:T(8,128)} custom-call(f32[16,5,8,128]{3,2,1,0:T(8,128)S(1)} %all-to-all-done.packet_ref, f32[768,128]{1,0:T(8,128)S(1)} %vote_stage.2.refs_0_), custom_call_target="tpu_custom_call" | custom-call | flops 20000000 | bytes 400000 | tf_op jit(solution)/shard_map/vote_stage/pallas_call | solution.py:361
  38.8 2.3 %collective-permute-done.1.refs_3_ = f32[320,128]{1,0:T(8,128)S(1)} collective-permute-done((f32[320,128]{1,0:T(8,128)S(1)}, f32[320,128]{1,0:T(8,128)S(1)}, u32[]{:S(2)}, u32[]{:S(2)}) %collective-permute-start.1) | collective-permute-done | bytes 163872 | tf_op jit(solution)/shard_map/ppermute | solution.py:501
  41.1 0.0 collective-permute-start.6
  41.1 0.0 collective-permute-done.3.refs_4_
  41.1 0.0 collective-permute-done.5.refs_6_
  41.1 0.0 collective-permute-done.4.refs_5_
  41.1 1.4 %collective-permute-done.6.refs_7_ = f32[320,128]{1,0:T(8,128)S(1)} collective-permute-done((f32[320,128]{1,0:T(8,128)S(1)}, f32[320,128]{1,0:T(8,128)S(1)}, u32[]{:S(2)}, u32[]{:S(2)}) %collective-permute-start.6) | collective-permute-done | bytes 163872 | tf_op jit(solution)/shard_map/ppermute | solution.py:510
  42.5 1.2 %place_stage.1 = f32[1280,256]{1,0:T(8,128)} custom-call(s32[1]{0:T(128)} %bitcast.8.where_ref, f32[320,128]{1,0:T(8,128)S(1)} %gain_stage.1.refs_0_, f32[320,128]{1,0:T(8,128)S(1)} %collective-permute-done.refs_1_, f32[320,128]{1,0:T(8,128)S(1)} %collective-permute-done.2.refs_2_, f32[320,128]{1,0:T(8,128)S(1)} %collective-permute-done.1.refs_3_, ...), custom_call_target="tpu_custom_call" | custom-call | tf_op jit(solution)/shard_map/place_stage/pallas_call | solution.py:428
Async XLA Ops:
  4.9 18.5 %all-to-all-start = ((f32[16,5,8,128]{3,2,1,0:T(8,128)}), f32[16,5,8,128]{3,2,1,0:T(8,128)S(1)}, u32[]{:S(2)}, u32[]{:S(2)}) async-start(f32[16,5,8,128]{3,2,1,0:T(8,128)} %get-tuple-element.13), calls=%async_computation | async-start | bytes 655360 | tf_op jit(solution)/shard_map/all_to_all | solution.py:485
  29.1 6.7 %collective-permute-start = (f32[320,128]{1,0:T(8,128)S(1)}, f32[320,128]{1,0:T(8,128)S(1)}, u32[]{:S(2)}, u32[]{:S(2)}) collective-permute-start(f32[320,128]{1,0:T(8,128)S(1)} %gain_stage.1.refs_0_), channel_id=1, source_target_pairs={{0,4},{1,3},{2,6},{3,1},{4,0},{5,7},{6,2},{7,5},{8,12},{9,11},{10,... | collective-permute-start | bytes 491528 | tf_op jit(solution)/shard_map/ppermute | solution.py:501
  29.3 7.0 %collective-permute-start.2 = (f32[320,128]{1,0:T(8,128)S(1)}, f32[320,128]{1,0:T(8,128)S(1)}, u32[]{:S(2)}, u32[]{:S(2)}) collective-permute-start(f32[320,128]{1,0:T(8,128)S(1)} %gain_stage.1.refs_0_), channel_id=1, source_target_pairs={{0,2},{1,5},{2,0},{3,7},{4,6},{5,1},{6,4},{7,3},{8,10},{9,13},{10,... | collective-permute-start | bytes 491528 | tf_op jit(solution)/shard_map/ppermute | solution.py:501
  35.8 5.3 %collective-permute-start.1 = (f32[320,128]{1,0:T(8,128)S(1)}, f32[320,128]{1,0:T(8,128)S(1)}, u32[]{:S(2)}, u32[]{:S(2)}) collective-permute-start(f32[320,128]{1,0:T(8,128)S(1)} %collective-permute-done.refs_1_), channel_id=1, source_target_pairs={{0,2},{1,5},{2,0},{3,7},{4,6},{5,1},{6,4},{7,3},{8,10},{9,13},{10,... | collective-permute-start | bytes 491528 | tf_op jit(solution)/shard_map/ppermute | solution.py:501
  35.8 5.3 %collective-permute-start.3 = (f32[320,128]{1,0:T(8,128)S(1)}, f32[320,128]{1,0:T(8,128)S(1)}, u32[]{:S(2)}, u32[]{:S(2)}) collective-permute-start(f32[320,128]{1,0:T(8,128)S(1)} %gain_stage.1.refs_0_), channel_id=1, source_target_pairs={{0,1},{1,0},{2,3},{3,2},{4,5},{5,4},{6,7},{7,6},{8,9},{9,8},{10,11... | collective-permute-start | bytes 491528 | tf_op jit(solution)/shard_map/ppermute | solution.py:510
  35.8 5.3 %collective-permute-start.4 = (f32[320,128]{1,0:T(8,128)S(1)}, f32[320,128]{1,0:T(8,128)S(1)}, u32[]{:S(2)}, u32[]{:S(2)}) collective-permute-start(f32[320,128]{1,0:T(8,128)S(1)} %collective-permute-done.refs_1_), channel_id=1, source_target_pairs={{0,1},{1,0},{2,3},{3,2},{4,5},{5,4},{6,7},{7,6},{8,9},{9,8},{10,11... | collective-permute-start | bytes 491528 | tf_op jit(solution)/shard_map/ppermute | solution.py:510
  36.3 4.8 %collective-permute-start.5 = (f32[320,128]{1,0:T(8,128)S(1)}, f32[320,128]{1,0:T(8,128)S(1)}, u32[]{:S(2)}, u32[]{:S(2)}) collective-permute-start(f32[320,128]{1,0:T(8,128)S(1)} %collective-permute-done.2.refs_2_), channel_id=1, source_target_pairs={{0,1},{1,0},{2,3},{3,2},{4,5},{5,4},{6,7},{7,6},{8,9},{9,8},{10,11... | collective-permute-start | bytes 491528 | tf_op jit(solution)/shard_map/ppermute | solution.py:510
  41.1 1.4 %collective-permute-start.6 = (f32[320,128]{1,0:T(8,128)S(1)}, f32[320,128]{1,0:T(8,128)S(1)}, u32[]{:S(2)}, u32[]{:S(2)}) collective-permute-start(f32[320,128]{1,0:T(8,128)S(1)} %collective-permute-done.1.refs_3_), channel_id=1, source_target_pairs={{0,1},{1,0},{2,3},{3,2},{4,5},{5,4},{6,7},{7,6},{8,9},{9,8},{10,11... | collective-permute-start | bytes 491528 | tf_op jit(solution)/shard_map/ppermute | solution.py:510

commit v4 on v3

--- a/solution.py
+++ b/solution.py
@@ -94,10 +94,32 @@
     group = 8 if leaves % 8 == 0 else leaves
     per_row = LANES // leaves
 
-    def body(bins_ref, leaf_ref, score_ref, level_ref, rank_ref, length_ref, votes_ref,
-             elected_ref, grad_ref, hess_ref, packet_ref, square, chosen_ref, bins_here, arrived):
-        fetch = pltpu.make_async_copy(bins_ref, bins_here, arrived)
-        fetch.start()
+    piece = round_up(cdiv(features, 4), 8)
+    cuts = [(f, min(piece, features - f)) for f in range(0, features, piece)]
+
+    def body(*refs):
+        sources = refs[0:8]
+        grad_ref, hess_ref, packet_ref = refs[8:11]
+        square, chosen_ref = refs[11:13]
+        copied = refs[13:21]
+        arrived = refs[21]
+        bins_here, leaf_ref, score_ref, level_ref, rank_ref, length_ref, votes_ref, elected_ref = (
+            copied
+        )
+        small = [
+            pltpu.make_async_copy(sources[k], copied[k], arrived.at[len(cuts) + k - 1])
+            for k in (5, 2, 3, 4, 7, 1, 6)
+        ]
+        fetches = [
+            pltpu.make_async_copy(
+                sources[0].at[pl.ds(f, size), :], bins_here.at[pl.ds(f, size), :], arrived.at[k]
+            )
+            for k, (f, size) in enumerate(cuts)
+        ]
+        for copy in small + fetches:
+            copy.start()
+        for copy in small:
+            copy.wait()
         square[...] = jnp.zeros(square.shape, jnp.float32)
         square[0:leaves, 0:picked] = elected_ref[...].astype(jnp.float32)
         elected_t = square[...].T
@@ -124,7 +146,8 @@
         shared = compact(jnp.concatenate(shared, axis=0))[0 : rows - picks]
         shared = jnp.where(lane < starts[-1], shared, 0.0)
         count = jnp.zeros((1, LANES), jnp.float32) + starts[-1].astype(jnp.float32)
-        fetch.wait()
+        for fetch in fetches:
+            fetch.wait()
         table = bins_here[...].astype(jnp.float32).astype(jnp.bfloat16)
         feature = lax.broadcasted_iota(jnp.int32, (padded, features), 1).astype(jnp.float32)
         chosen = jnp.zeros((padded, documents), jnp.float32)
@@ -167,10 +190,7 @@
     vmem = pl.BlockSpec(memory_space=pltpu.VMEM)
     return pl.pallas_call(
         body,
-        in_specs=[pl.BlockSpec(memory_space=pltpu.HBM)]
-        + [vmem] * 4
-        + [pl.BlockSpec(memory_space=pltpu.SMEM)]
-        + [vmem] * 2,
+        in_specs=[pl.BlockSpec(memory_space=pltpu.HBM)] * 8,
         out_specs=[vmem] * 3,
         out_shape=[
             jax.ShapeDtypeStruct((1, documents), jnp.float32),
@@ -183,7 +203,14 @@
             pltpu.VMEM((LANES, LANES), jnp.float32),
             pltpu.VMEM((padded, documents), jnp.float32),
             pltpu.VMEM((features, documents), jnp.int32),
-            pltpu.SemaphoreType.DMA,
+            pltpu.VMEM((1, documents), jnp.int32),
+            pltpu.VMEM((1, documents), jnp.float32),
+            pltpu.VMEM((1, documents), jnp.int32),
+            pltpu.VMEM((1, documents), jnp.int32),
+            pltpu.SMEM(lengths.shape, jnp.int32),
+            pltpu.VMEM(votes.shape, jnp.int32),
+            pltpu.VMEM(elected.shape, jnp.int32),
+            pltpu.SemaphoreType.DMA((len(cuts) + 7,)),
         ],
         compiler_params=pltpu.CompilerParams(vmem_limit_bytes=48 << 20),
         name="local_stage",
@@ -200,7 +227,7 @@
 
     half = cdiv(chunks, 2)
 
-    def body(where_ref, packet_ref, out_ref, total_ref, grad_ref, hess_ref):
+    def body(where_ref, packet_ref, out_ref, total_ref, grad_ref, hess_ref, late_ref):
         leaf_id = lax.broadcasted_iota(jnp.int32, (leaves, LANES), 0).astype(jnp.float32)
         bin_id = lax.broadcasted_iota(jnp.int32, (LANES, LANES), 0).astype(jnp.float32)
         local = []
@@ -264,20 +291,19 @@
         total_ref[...] = total
         grad_ref[...] = grad_all
         hess_ref[...] = hess_all
-        for s0 in range(0, devices, 16):
-            flag = flags[s0 // 16]
-
-            def late(k, carry, s0=s0, flag=flag):
-                @pl.when((jnp.right_shift(flag, k) & 1) == 1)
-                def _():
-                    more, grad_more, hess_more = terms([s0 + k], range(half, chunks))
-                    total_ref[...] += more
-                    grad_ref[...] += grad_more
-                    hess_ref[...] += hess_more
-
-                return carry
-
-            lax.fori_loop(0, min(16, devices - s0), late, 0)
+        late = jnp.int32(0)
+        for s in range(devices):
+            late_ref[late] = s
+            late = late + (jnp.right_shift(flags[s // 16], s % 16) & 1)
+
+        def add(k, carry):
+            more, grad_more, hess_more = terms([late_ref[k]], range(half, chunks))
+            total_ref[...] += more
+            grad_ref[...] += grad_more
+            hess_ref[...] += hess_more
+            return carry
+
+        lax.fori_loop(0, late, add, 0)
         total = total_ref[...]
         grad_all = grad_ref[...]
         hess_all = hess_ref[...]
@@ -305,6 +331,7 @@
             pltpu.VMEM((4 * leaves, units * LANES), jnp.float32),
             pltpu.VMEM((leaves, LANES), jnp.float32),
             pltpu.VMEM((leaves, LANES), jnp.float32),
+            pltpu.SMEM((devices + 1,), jnp.int32),
         ],
         compiler_params=pltpu.CompilerParams(vmem_limit_bytes=48 << 20),
         name="gain_stage",

time: 43.2 us -> 42.5 us (0.984); the launches traced: 43.6 us -> 42.4 us
  Pallas kernels: 15.4 us -> 14.2 us
    pallas_call x1, Pallas kernels: 5.68 us -> 4.83 us  [gain_stage(): pl.pallas_call(body, in_specs=[pl.BlockSpec(memory_space=pltpu.SMEM), vme...]
where the time goes in v4:
time: 42.5 us; the launch traced here: 42.4 us
  waiting for transfers between devices  18.1 us (43%)
  Pallas kernels  14.2 us (33%)
  starting transfers between devices  9.41 us (22%)
  between operations  0.68 us (2%)
    all_to_all x1, waiting for transfers between devices, on_device(): received = lax.all_to_all(packets, 'rows', 0, 0)  11.1 us
    all_to_all x1, starting transfers between devices, on_device(): received = lax.all_to_all(packets, 'rows', 0, 0)  7.43 us
    ppermute x3, waiting for transfers between devices, on_device(): moved = [lax.ppermute(b, 'rows', pairs[p]) for b in blocks]  5.69 us
    pallas_call x1, Pallas kernels, gain_stage(): pl.pallas_call(body, in_specs=[pl.BlockSpec(memory_space=pltpu.SMEM), vme...  4.83 us
    pallas_call x2, Pallas kernels, vote_stage(): pl.pallas_call(body, in_specs=[vmem] * len(inputs), out_specs=vmem, out_s...  4.33 us
    pallas_call x1, Pallas kernels, local_stage(): pl.pallas_call(body, in_specs=[pl.BlockSpec(memory_space=pltpu.HBM)] * 8,...  3.86 us
    ppermute x3, starting transfers between devices, on_device(): moved = [lax.ppermute(b, 'rows', pairs[p]) for b in blocks]  1.46 us
    ppermute x4, waiting for transfers between devices, on_device(): blocks = blocks + [lax.ppermute(b, 'rows', sibling) for b in blocks]  1.38 us
  transfers between devices with their start and end apart: 8, of which 4 were waited for; matrix products, arithmetic and copies ran while one was open for 0% of the time, Pallas kernels for 10%

profile of v4, /device:TPU:0, one launch (start us, length us, event | category | flops | bytes accessed | tf_op | source)
XLA Modules:
  0.0 42.4 jit_solution(465249513380635653)
XLA Ops:
  0.6 3.9 %local_stage.1 = (f32[1,512]{1,0:T(1,128)}, f32[1,512]{1,0:T(1,128)}, f32[16,5,8,128]{3,2,1,0:T(8,128)}) custom-call(s32[700,512]{1,0:T(8,128)} %bitcast.10, s32[1,512]{1,0:T(1,128)} %bitcast.13, f32[1,512]{1,0:T(1,128)} %bitcast.14, s32[1,512]{1,0:T(1,128)} %bitcast.15, s32[1,512]{1,0:T(1,128)} %bitcast.16, s32[2]{0:T(128)} %refs_5_.1, ...), custom_call_target="tpu_custom_call" | custom-call | tf_op jit(solution)/shard_map/local_stage/pallas_call | solution.py:191
  4.5 7.4 %all-to-all-start = ((f32[16,5,8,128]{3,2,1,0:T(8,128)}), f32[16,5,8,128]{3,2,1,0:T(8,128)S(1)}, u32[]{:S(2)}, u32[]{:S(2)}) async-start(f32[16,5,8,128]{3,2,1,0:T(8,128)} %get-tuple-element.13), calls=%async_computation | async-start | bytes 655360 | tf_op jit(solution)/shard_map/all_to_all | solution.py:512
  11.9 11.1 %all-to-all-done.packet_ref = f32[16,5,8,128]{3,2,1,0:T(8,128)S(1)} async-done(((f32[16,5,8,128]{3,2,1,0:T(8,128)}), f32[16,5,8,128]{3,2,1,0:T(8,128)S(1)}, u32[]{:S(2)}, u32[]{:S(2)}) %all-to-all-start) | async-done | bytes 327712 | tf_op jit(solution)/shard_map/all_to_all | solution.py:512
  23.0 4.8 %gain_stage.1.refs_0_ = f32[320,128]{1,0:T(8,128)S(1)} custom-call(s32[1]{0:T(128)} %bitcast.8.where_ref, f32[16,5,8,128]{3,2,1,0:T(8,128)S(1)} %all-to-all-done.packet_ref), custom_call_target="tpu_custom_call" | custom-call | tf_op jit(solution)/shard_map/gain_stage/pallas_call | solution.py:325
  27.8 0.2 collective-permute-start
  28.1 1.2 %collective-permute-start.2 = (f32[320,128]{1,0:T(8,128)S(1)}, f32[320,128]{1,0:T(8,128)S(1)}, u32[]{:S(2)}, u32[]{:S(2)}) collective-permute-start(f32[320,128]{1,0:T(8,128)S(1)} %gain_stage.1.refs_0_), channel_id=1, source_target_pairs={{0,2},{1,5},{2,0},{3,7},{4,6},{5,1},{6,4},{7,3},{8,10},{9,13},{10,... | collective-permute-start | bytes 491528 | tf_op jit(solution)/shard_map/ppermute | solution.py:528
  29.3 1.8 %vote_stage.2.refs_0_ = f32[768,128]{1,0:T(8,128)S(1)} custom-call(f32[16,5,8,128]{3,2,1,0:T(8,128)S(1)} %all-to-all-done.packet_ref), custom_call_target="tpu_custom_call" | custom-call | flops 20000000 | bytes 400000 | tf_op jit(solution)/shard_map/vote_stage/pallas_call | solution.py:388
  31.1 3.4 %collective-permute-done.refs_1_ = f32[320,128]{1,0:T(8,128)S(1)} collective-permute-done((f32[320,128]{1,0:T(8,128)S(1)}, f32[320,128]{1,0:T(8,128)S(1)}, u32[]{:S(2)}, u32[]{:S(2)}) %collective-permute-start) | collective-permute-done | bytes 163872 | tf_op jit(solution)/shard_map/ppermute | solution.py:528
  34.5 0.0 collective-permute-start.1
  34.5 0.0 collective-permute-start.3
  34.5 0.5 %collective-permute-start.4 = (f32[320,128]{1,0:T(8,128)S(1)}, f32[320,128]{1,0:T(8,128)S(1)}, u32[]{:S(2)}, u32[]{:S(2)}) collective-permute-start(f32[320,128]{1,0:T(8,128)S(1)} %collective-permute-done.refs_1_), channel_id=1, source_target_pairs={{0,1},{1,0},{2,3},{3,2},{4,5},{5,4},{6,7},{7,6},{8,9},{9,8},{10,11... | collective-permute-start | bytes 491528 | tf_op jit(solution)/shard_map/ppermute | solution.py:537
  35.0 0.0 collective-permute-done.2.refs_2_
  35.0 0.0 collective-permute-start.5
  35.0 2.5 %vote_stage.3 = s32[32,700]{1,0:T(8,128)} custom-call(f32[16,5,8,128]{3,2,1,0:T(8,128)S(1)} %all-to-all-done.packet_ref, f32[768,128]{1,0:T(8,128)S(1)} %vote_stage.2.refs_0_), custom_call_target="tpu_custom_call" | custom-call | flops 20000000 | bytes 400000 | tf_op jit(solution)/shard_map/vote_stage/pallas_call | solution.py:388
  37.6 2.3 %collective-permute-done.1.refs_3_ = f32[320,128]{1,0:T(8,128)S(1)} collective-permute-done((f32[320,128]{1,0:T(8,128)S(1)}, f32[320,128]{1,0:T(8,128)S(1)}, u32[]{:S(2)}, u32[]{:S(2)}) %collective-permute-start.1) | collective-permute-done | bytes 163872 | tf_op jit(solution)/shard_map/ppermute | solution.py:528
  39.8 0.0 collective-permute-start.6
  39.8 0.0 collective-permute-done.3.refs_4_
  39.8 0.0 collective-permute-done.5.refs_6_
  39.9 0.0 collective-permute-done.4.refs_5_
  39.9 1.4 %collective-permute-done.6.refs_7_ = f32[320,128]{1,0:T(8,128)S(1)} collective-permute-done((f32[320,128]{1,0:T(8,128)S(1)}, f32[320,128]{1,0:T(8,128)S(1)}, u32[]{:S(2)}, u32[]{:S(2)}) %collective-permute-start.6) | collective-permute-done | bytes 163872 | tf_op jit(solution)/shard_map/ppermute | solution.py:537
  41.2 1.2 %place_stage.1 = f32[1280,256]{1,0:T(8,128)} custom-call(s32[1]{0:T(128)} %bitcast.8.where_ref, f32[320,128]{1,0:T(8,128)S(1)} %gain_stage.1.refs_0_, f32[320,128]{1,0:T(8,128)S(1)} %collective-permute-done.refs_1_, f32[320,128]{1,0:T(8,128)S(1)} %collective-permute-done.2.refs_2_, f32[320,128]{1,0:T(8,128)S(1)} %collective-permute-done.1.refs_3_, ...), custom_call_target="tpu_custom_call" | custom-call | tf_op jit(solution)/shard_map/place_stage/pallas_call | solution.py:455
Async XLA Ops:
  4.5 18.5 %all-to-all-start = ((f32[16,5,8,128]{3,2,1,0:T(8,128)}), f32[16,5,8,128]{3,2,1,0:T(8,128)S(1)}, u32[]{:S(2)}, u32[]{:S(2)}) async-start(f32[16,5,8,128]{3,2,1,0:T(8,128)} %get-tuple-element.13), calls=%async_computation | async-start | bytes 655360 | tf_op jit(solution)/shard_map/all_to_all | solution.py:512
  27.8 6.7 %collective-permute-start = (f32[320,128]{1,0:T(8,128)S(1)}, f32[320,128]{1,0:T(8,128)S(1)}, u32[]{:S(2)}, u32[]{:S(2)}) collective-permute-start(f32[320,128]{1,0:T(8,128)S(1)} %gain_stage.1.refs_0_), channel_id=1, source_target_pairs={{0,4},{1,3},{2,6},{3,1},{4,0},{5,7},{6,2},{7,5},{8,12},{9,11},{10,... | collective-permute-start | bytes 491528 | tf_op jit(solution)/shard_map/ppermute | solution.py:528
  28.1 7.0 %collective-permute-start.2 = (f32[320,128]{1,0:T(8,128)S(1)}, f32[320,128]{1,0:T(8,128)S(1)}, u32[]{:S(2)}, u32[]{:S(2)}) collective-permute-start(f32[320,128]{1,0:T(8,128)S(1)} %gain_stage.1.refs_0_), channel_id=1, source_target_pairs={{0,2},{1,5},{2,0},{3,7},{4,6},{5,1},{6,4},{7,3},{8,10},{9,13},{10,... | collective-permute-start | bytes 491528 | tf_op jit(solution)/shard_map/ppermute | solution.py:528
  34.5 5.3 %collective-permute-start.1 = (f32[320,128]{1,0:T(8,128)S(1)}, f32[320,128]{1,0:T(8,128)S(1)}, u32[]{:S(2)}, u32[]{:S(2)}) collective-permute-start(f32[320,128]{1,0:T(8,128)S(1)} %collective-permute-done.refs_1_), channel_id=1, source_target_pairs={{0,2},{1,5},{2,0},{3,7},{4,6},{5,1},{6,4},{7,3},{8,10},{9,13},{10,... | collective-permute-start | bytes 491528 | tf_op jit(solution)/shard_map/ppermute | solution.py:528
  34.5 5.3 %collective-permute-start.3 = (f32[320,128]{1,0:T(8,128)S(1)}, f32[320,128]{1,0:T(8,128)S(1)}, u32[]{:S(2)}, u32[]{:S(2)}) collective-permute-start(f32[320,128]{1,0:T(8,128)S(1)} %gain_stage.1.refs_0_), channel_id=1, source_target_pairs={{0,1},{1,0},{2,3},{3,2},{4,5},{5,4},{6,7},{7,6},{8,9},{9,8},{10,11... | collective-permute-start | bytes 491528 | tf_op jit(solution)/shard_map/ppermute | solution.py:537
  34.5 5.3 %collective-permute-start.4 = (f32[320,128]{1,0:T(8,128)S(1)}, f32[320,128]{1,0:T(8,128)S(1)}, u32[]{:S(2)}, u32[]{:S(2)}) collective-permute-start(f32[320,128]{1,0:T(8,128)S(1)} %collective-permute-done.refs_1_), channel_id=1, source_target_pairs={{0,1},{1,0},{2,3},{3,2},{4,5},{5,4},{6,7},{7,6},{8,9},{9,8},{10,11... | collective-permute-start | bytes 491528 | tf_op jit(solution)/shard_map/ppermute | solution.py:537
  35.0 4.8 %collective-permute-start.5 = (f32[320,128]{1,0:T(8,128)S(1)}, f32[320,128]{1,0:T(8,128)S(1)}, u32[]{:S(2)}, u32[]{:S(2)}) collective-permute-start(f32[320,128]{1,0:T(8,128)S(1)} %collective-permute-done.2.refs_2_), channel_id=1, source_target_pairs={{0,1},{1,0},{2,3},{3,2},{4,5},{5,4},{6,7},{7,6},{8,9},{9,8},{10,11... | collective-permute-start | bytes 491528 | tf_op jit(solution)/shard_map/ppermute | solution.py:537
  39.8 1.4 %collective-permute-start.6 = (f32[320,128]{1,0:T(8,128)S(1)}, f32[320,128]{1,0:T(8,128)S(1)}, u32[]{:S(2)}, u32[]{:S(2)}) collective-permute-start(f32[320,128]{1,0:T(8,128)S(1)} %collective-permute-done.1.refs_3_), channel_id=1, source_target_pairs={{0,1},{1,0},{2,3},{3,2},{4,5},{5,4},{6,7},{7,6},{8,9},{9,8},{10,11... | collective-permute-start | bytes 491528 | tf_op jit(solution)/shard_map/ppermute | solution.py:537

commit v5 on v4

--- a/solution.py
+++ b/solution.py
@@ -102,7 +102,7 @@
         grad_ref, hess_ref, packet_ref = refs[8:11]
         square, chosen_ref = refs[11:13]
         copied = refs[13:21]
-        arrived = refs[21]
+        arrived, hot_ref = refs[21:23]
         bins_here, leaf_ref, score_ref, level_ref, rank_ref, length_ref, votes_ref, elected_ref = (
             copied
         )
@@ -146,16 +146,20 @@
         shared = compact(jnp.concatenate(shared, axis=0))[0 : rows - picks]
         shared = jnp.where(lane < starts[-1], shared, 0.0)
         count = jnp.zeros((1, LANES), jnp.float32) + starts[-1].astype(jnp.float32)
-        for fetch in fetches:
-            fetch.wait()
-        table = bins_here[...].astype(jnp.float32).astype(jnp.bfloat16)
         feature = lax.broadcasted_iota(jnp.int32, (padded, features), 1).astype(jnp.float32)
-        chosen = jnp.zeros((padded, documents), jnp.float32)
         for first in range(0, leaves, group):
             hot = []
             for l in range(first, first + group):
                 hot.append((elected_t[0:padded, l : l + 1] == feature).astype(jnp.float32))
-            hot = jnp.concatenate(hot, axis=0).astype(jnp.bfloat16)
+            hot_ref[first * padded : (first + group) * padded, :] = jnp.concatenate(
+                hot, axis=0
+            ).astype(jnp.bfloat16)
+        for fetch in fetches:
+            fetch.wait()
+        table = bins_here[...].astype(jnp.float32).astype(jnp.bfloat16)
+        chosen = jnp.zeros((padded, documents), jnp.float32)
+        for first in range(0, leaves, group):
+            hot = hot_ref[first * padded : (first + group) * padded, :]
             found = jnp.dot(hot, table, preferred_element_type=jnp.float32)
             for i in range(group):
                 chosen = jnp.where(
@@ -211,6 +215,7 @@
             pltpu.VMEM(votes.shape, jnp.int32),
             pltpu.VMEM(elected.shape, jnp.int32),
             pltpu.SemaphoreType.DMA((len(cuts) + 7,)),
+            pltpu.VMEM((leaves * padded, features), jnp.bfloat16),
         ],
         compiler_params=pltpu.CompilerParams(vmem_limit_bytes=48 << 20),
         name="local_stage",
@@ -226,6 +231,7 @@
     even = units % HALVES == 0
 
     half = cdiv(chunks, 2)
+    batch = 4
 
     def body(where_ref, packet_ref, out_ref, total_ref, grad_ref, hess_ref, late_ref):
         leaf_id = lax.broadcasted_iota(jnp.int32, (leaves, LANES), 0).astype(jnp.float32)
@@ -241,30 +247,30 @@
             else:
                 local.append(jnp.clip((base + i) // HALVES - first, 0, picks - 1))
                 limit.append(bin_id + ((base + i) % HALVES * LANES).astype(jnp.float32))
-        def terms(sources, parts):
+        def terms(tiles):
             weights = []
             steps = [[] for _ in range(units)]
             grad_sum = jnp.zeros((leaves, LANES), jnp.float32)
             hess_sum = jnp.zeros((leaves, LANES), jnp.float32)
-            for s in sources:
-                for c in parts:
-                    mine = packet_ref[s, c, picks : picks + 1, :] == leaf_id
-                    grad = jnp.where(mine, packet_ref[s, c, picks + 1 : picks + 2, :], 0.0)
-                    hess = jnp.where(mine, packet_ref[s, c, picks + 2 : picks + 3, :], 0.0)
-                    grad_sum = grad_sum + grad
-                    hess_sum = hess_sum + hess
-                    grad_high = grad.astype(jnp.bfloat16)
-                    hess_high = hess.astype(jnp.bfloat16)
-                    grad_low = (grad - grad_high.astype(jnp.float32)).astype(jnp.bfloat16)
-                    hess_low = (hess - hess_high.astype(jnp.float32)).astype(jnp.bfloat16)
-                    weights.append(
-                        jnp.concatenate([grad_high, hess_high, grad_low, hess_low], axis=0)
-                    )
-                    for i in range(units):
-                        value = packet_ref[s, c, pl.ds(local[i], 1), :]
-                        steps[i].append(
-                            (value <= limit[i]).astype(jnp.float32).astype(jnp.bfloat16)
-                        )
+            for s, c, valid in tiles:
+                owner = packet_ref[s, c, picks : picks + 1, :]
+                if valid is not None:
+                    owner = jnp.where(valid, owner, -1.0)
+                mine = owner == leaf_id
+                grad = jnp.where(mine, packet_ref[s, c, picks + 1 : picks + 2, :], 0.0)
+                hess = jnp.where(mine, packet_ref[s, c, picks + 2 : picks + 3, :], 0.0)
+                grad_sum = grad_sum + grad
+                hess_sum = hess_sum + hess
+                grad_high = grad.astype(jnp.bfloat16)
+                hess_high = hess.astype(jnp.bfloat16)
+                grad_low = (grad - grad_high.astype(jnp.float32)).astype(jnp.bfloat16)
+                hess_low = (hess - hess_high.astype(jnp.float32)).astype(jnp.bfloat16)
+                weights.append(
+                    jnp.concatenate([grad_high, hess_high, grad_low, hess_low], axis=0)
+                )
+                for i in range(units):
+                    value = packet_ref[s, c, pl.ds(local[i], 1), :]
+                    steps[i].append((value <= limit[i]).astype(jnp.float32).astype(jnp.bfloat16))
             weight = jnp.concatenate(weights, axis=1)
             step = jnp.concatenate([jnp.concatenate(p, axis=1) for p in steps], axis=0)
             product = lax.dot_general(
@@ -272,38 +278,53 @@
             )
             return product, grad_sum, hess_sum
 
-        flags = []
-        for s0 in range(0, devices, 16):
-            flag = jnp.zeros((1, LANES), jnp.float32)
-            for s in range(s0, min(s0 + 16, devices)):
-                row = plan["vote_lines"]
-                count = packet_ref[s, chunks + row // plan["rows"], row % plan["rows"], :]
-                flag = flag + jnp.where(
-                    count.reshape(1, LANES) > float(half * LANES), float(1 << (s - s0)), 0.0
-                )
-            flags.append(jnp.max(flag).astype(jnp.int32))
-        total, grad_all, hess_all = terms(range(chunk), range(half))
-        for s0 in range(chunk, devices, chunk):
-            more, grad_more, hess_more = terms(range(s0, s0 + chunk), range(half))
-            total = total + more
-            grad_all = grad_all + grad_more
-            hess_all = hess_all + hess_more
+        late = jnp.int32(0)
+        for c in range(half, chunks):
+            for s0 in range(0, devices, 16):
+                flag = jnp.zeros((1, LANES), jnp.float32)
+                for s in range(s0, min(s0 + 16, devices)):
+                    row = plan["vote_lines"]
+                    count = packet_ref[s, chunks + row // plan["rows"], row % plan["rows"], :]
+                    flag = flag + jnp.where(
+                        count.reshape(1, LANES) > float(c * LANES), float(1 << (s - s0)), 0.0
+                    )
+                flag = jnp.max(flag).astype(jnp.int32)
+                for s in range(s0, min(s0 + 16, devices)):
+                    late_ref[late] = s * chunks + c
+                    late = late + (jnp.right_shift(flag, s - s0) & 1)
+
+        def listed(first):
+            tiles = []
+            for k in range(batch):
+                valid = first + k < late
+                tile = jnp.where(valid, late_ref[first + k], 0)
+                tiles.append((tile // chunks, tile % chunks, valid))
+            return tiles
+
+        total = grad_all = hess_all = None
+        for s0 in range(0, devices + 1, chunk):
+            if s0 < devices:
+                tiles = [(s, c, None) for s in range(s0, s0 + chunk) for c in range(half)]
+            else:
+                tiles = listed(0)
+            more, grad_more, hess_more = terms(tiles)
+            if s0:
+                more = total + more
+                grad_more = grad_all + grad_more
+                hess_more = hess_all + hess_more
+            total, grad_all, hess_all = more, grad_more, hess_more
         total_ref[...] = total
         grad_ref[...] = grad_all
         hess_ref[...] = hess_all
-        late = jnp.int32(0)
-        for s in range(devices):
-            late_ref[late] = s
-            late = late + (jnp.right_shift(flags[s // 16], s % 16) & 1)
 
         def add(k, carry):
-            more, grad_more, hess_more = terms([late_ref[k]], range(half, chunks))
+            more, grad_more, hess_more = terms(listed(k * batch))
             total_ref[...] += more
             grad_ref[...] += grad_more
             hess_ref[...] += hess_more
             return carry
 
-        lax.fori_loop(0, late, add, 0)
+        lax.fori_loop(1, jnp.maximum((late + batch - 1) // batch, 1), add, 0)
         total = total_ref[...]
         grad_all = grad_ref[...]
         hess_all = hess_ref[...]
@@ -331,7 +352,7 @@
             pltpu.VMEM((4 * leaves, units * LANES), jnp.float32),
             pltpu.VMEM((leaves, LANES), jnp.float32),
             pltpu.VMEM((leaves, LANES), jnp.float32),
-            pltpu.SMEM((devices + 1,), jnp.int32),
+            pltpu.SMEM((devices * chunks + batch,), jnp.int32),
         ],
         compiler_params=pltpu.CompilerParams(vmem_limit_bytes=48 << 20),
         name="gain_stage",
@@ -522,19 +543,30 @@
                 [(i, i ^ (twin[p] if i & 1 else far[p])) for i in range(devices)]
                 for p in range(len(far))
             ]
-            blocks = [block]
             tags = [(0, 0)]
             for p in range(len(far)):
-                moved = [lax.ppermute(b, "rows", pairs[p]) for b in blocks]
+                tags = tags + [(even | far[p], odd | twin[p]) for even, odd in tags]
+            sibling = [(i, i ^ 1) for i in range(devices)]
+
+            def send(b, pair):
+                return lax.ppermute(b, "rows", pair)
+
+            moved = send(block, pairs[0])
+            again, votes = lax.optimization_barrier((block, votes))
+            crossed = [send(again, sibling)]
+            moved, votes = lax.optimization_barrier((moved, votes))
+            blocks = [block, moved]
+            for p in range(1, len(far)):
+                moved = [send(b, pairs[p]) for b in [again] + blocks[1:]]
                 if p == len(far) - 1:
                     votes = vote_stage(received, votes, range(middle, devices), *count_args)
+                    waiting, votes = lax.optimization_barrier((blocks[1:] + moved[:-1], votes))
+                    crossed = crossed + [send(b, sibling) for b in waiting]
                     moved[-1], votes = lax.optimization_barrier((moved[-1], votes))
-                elif p == len(far) - 2:
-                    moved[0], votes = lax.optimization_barrier((moved[0], votes))
                 blocks = blocks + moved
-                tags = tags + [(even | far[p], odd | twin[p]) for even, odd in tags]
-            sibling = [(i, i ^ 1) for i in range(devices)]
-            blocks = blocks + [lax.ppermute(b, "rows", sibling) for b in blocks]
+            if len(far) == 1:
+                votes = vote_stage(received, votes, range(middle, devices), *count_args)
+            blocks = blocks + crossed + [send(blocks[-1], sibling)]
             plan["tags"] = tags
         else:
             votes = vote_stage(received, votes, range(middle, devices), *count_args)

time: 42.5 us -> 41.3 us (0.972)
  waiting for transfers between devices: 18.1 us -> 17.1 us
    ppermute x7, waiting for transfers between devices: 7.07 us -> 6.05 us  [send(): return lax.ppermute(b, 'rows', pair)]
    pallas_call x1, Pallas kernels: 4.83 us -> 4.12 us  [gain_stage(): pl.pallas_call(body, in_specs=[pl.BlockSpec(memory_space=pltpu.SMEM), vme...]
  transfers between devices with their start and end apart: 8 -> 8, of which waited for: 4 -> 4; matrix products, arithmetic and copies ran while one was open for 0% -> 0% of each run, Pallas kernels for 10% -> 11%
where the time goes in v5:
time: 41.3 us; the launch traced here: 41.1 us
  waiting for transfers between devices  17.1 us (41%)
  Pallas kernels  13.8 us (33%)
  starting transfers between devices  9.48 us (23%)
  between operations  0.68 us (2%)
    all_to_all x1, waiting for transfers between devices, on_device(): received = lax.all_to_all(packets, 'rows', 0, 0)  11.1 us
    all_to_all x1, starting transfers between devices, on_device(): received = lax.all_to_all(packets, 'rows', 0, 0)  7.43 us
    ppermute x7, waiting for transfers between devices, send(): return lax.ppermute(b, 'rows', pair)  6.05 us
    pallas_call x2, Pallas kernels, vote_stage(): pl.pallas_call(body, in_specs=[vmem] * len(inputs), out_specs=vmem, out_s...  4.33 us
    pallas_call x1, Pallas kernels, local_stage(): pl.pallas_call(body, in_specs=[pl.BlockSpec(memory_space=pltpu.HBM)] * 8,...  4.16 us
    pallas_call x1, Pallas kernels, gain_stage(): pl.pallas_call(body, in_specs=[pl.BlockSpec(memory_space=pltpu.SMEM), vme...  4.12 us
    ppermute x7, starting transfers between devices, send(): return lax.ppermute(b, 'rows', pair)  2.05 us
    pallas_call x1, Pallas kernels, place_stage(): pl.pallas_call(body, in_specs=[pl.BlockSpec(memory_space=pltpu.SMEM)] + [...  1.18 us
  transfers between devices with their start and end apart: 8, of which 4 were waited for; matrix products, arithmetic and copies ran while one was open for 0% of the time, Pallas kernels for 11%

profile of v5, /device:TPU:0, one launch (start us, length us, event | category | flops | bytes accessed | tf_op | source)
XLA Modules:
  0.0 41.1 jit_solution(7217395457887071850)
XLA Ops:
  0.6 4.2 %local_stage.1 = (f32[1,512]{1,0:T(1,128)}, f32[1,512]{1,0:T(1,128)}, f32[16,5,8,128]{3,2,1,0:T(8,128)}) custom-call(s32[700,512]{1,0:T(8,128)} %bitcast.10, s32[1,512]{1,0:T(1,128)} %bitcast.13, f32[1,512]{1,0:T(1,128)} %bitcast.14, s32[1,512]{1,0:T(1,128)} %bitcast.15, s32[1,512]{1,0:T(1,128)} %bitcast.16, s32[2]{0:T(128)} %refs_5_.1, ...), custom_call_target="tpu_custom_call" | custom-call | tf_op jit(solution)/shard_map/local_stage/pallas_call | solution.py:195
  4.8 7.4 %all-to-all-start = ((f32[16,5,8,128]{3,2,1,0:T(8,128)}), f32[16,5,8,128]{3,2,1,0:T(8,128)S(1)}, u32[]{:S(2)}, u32[]{:S(2)}) async-start(f32[16,5,8,128]{3,2,1,0:T(8,128)} %get-tuple-element.18), calls=%async_computation | async-start | bytes 655360 | tf_op jit(solution)/shard_map/all_to_all | solution.py:533
  12.2 11.1 %all-to-all-done.packet_ref = f32[16,5,8,128]{3,2,1,0:T(8,128)S(1)} async-done(((f32[16,5,8,128]{3,2,1,0:T(8,128)}), f32[16,5,8,128]{3,2,1,0:T(8,128)S(1)}, u32[]{:S(2)}, u32[]{:S(2)}) %all-to-all-start) | async-done | bytes 327712 | tf_op jit(solution)/shard_map/all_to_all | solution.py:533
  23.3 4.1 %gain_stage.1.refs_0_ = f32[320,128]{1,0:T(8,128)S(1)} custom-call(s32[1]{0:T(128)} %bitcast.8.where_ref, f32[16,5,8,128]{3,2,1,0:T(8,128)S(1)} %all-to-all-done.packet_ref), custom_call_target="tpu_custom_call" | custom-call | tf_op jit(solution)/shard_map/gain_stage/pallas_call | solution.py:346
  27.4 0.2 collective-permute-start
  27.7 1.8 %vote_stage.2.refs_0_ = f32[768,128]{1,0:T(8,128)S(1)} custom-call(f32[16,5,8,128]{3,2,1,0:T(8,128)S(1)} %all-to-all-done.packet_ref), custom_call_target="tpu_custom_call" | custom-call | flops 20000000 | bytes 400000 | tf_op jit(solution)/shard_map/vote_stage/pallas_call | solution.py:409
  29.5 1.3 %collective-permute-start.2 = (f32[320,128]{1,0:T(8,128)S(1)}, f32[320,128]{1,0:T(8,128)S(1)}, u32[]{:S(2)}, u32[]{:S(2)}) collective-permute-start(f32[320,128]{1,0:T(8,128)S(1)} %gain_stage.1.refs_0_), channel_id=1, source_target_pairs={{0,2},{1,5},{2,0},{3,7},{4,6},{5,1},{6,4},{7,3},{8,10},{9,13},{10,... | collective-permute-start | bytes 491528 | tf_op jit(solution)/shard_map/ppermute | solution.py:552
  30.8 2.4 %collective-permute-done.refs_1_ = f32[320,128]{1,0:T(8,128)S(1)} collective-permute-done((f32[320,128]{1,0:T(8,128)S(1)}, f32[320,128]{1,0:T(8,128)S(1)}, u32[]{:S(2)}, u32[]{:S(2)}) %collective-permute-start) | collective-permute-done | bytes 163872 | tf_op jit(solution)/shard_map/ppermute | solution.py:552
  33.2 0.0 collective-permute-start.1
  33.2 0.0 collective-permute-start.3
  33.2 2.5 %vote_stage.3 = s32[32,700]{1,0:T(8,128)} custom-call(f32[16,5,8,128]{3,2,1,0:T(8,128)S(1)} %all-to-all-done.packet_ref, f32[768,128]{1,0:T(8,128)S(1)} %vote_stage.2.refs_0_), custom_call_target="tpu_custom_call" | custom-call | flops 20000000 | bytes 400000 | tf_op jit(solution)/shard_map/vote_stage/pallas_call | solution.py:409
  35.7 0.0 collective-permute-done.2.refs_2_
  35.7 0.5 %collective-permute-start.4 = (f32[320,128]{1,0:T(8,128)S(1)}, f32[320,128]{1,0:T(8,128)S(1)}, u32[]{:S(2)}, u32[]{:S(2)}) collective-permute-start(f32[320,128]{1,0:T(8,128)S(1)} %collective-permute-done.refs_1_), channel_id=1, source_target_pairs={{0,1},{1,0},{2,3},{3,2},{4,5},{5,4},{6,7},{7,6},{8,9},{9,8},{10,11... | collective-permute-start | bytes 491528 | tf_op jit(solution)/shard_map/ppermute | solution.py:552
  36.2 0.0 collective-permute-start.5
  36.2 2.3 %collective-permute-done.1.refs_3_ = f32[320,128]{1,0:T(8,128)S(1)} collective-permute-done((f32[320,128]{1,0:T(8,128)S(1)}, f32[320,128]{1,0:T(8,128)S(1)}, u32[]{:S(2)}, u32[]{:S(2)}) %collective-permute-start.1) | collective-permute-done | bytes 163872 | tf_op jit(solution)/shard_map/ppermute | solution.py:552
  38.5 0.0 collective-permute-start.6
  38.5 0.0 collective-permute-done.3.refs_4_
  38.5 0.0 collective-permute-done.4.refs_5_
  38.5 0.0 collective-permute-done.5.refs_6_
  38.5 1.4 %collective-permute-done.6.refs_7_ = f32[320,128]{1,0:T(8,128)S(1)} collective-permute-done((f32[320,128]{1,0:T(8,128)S(1)}, f32[320,128]{1,0:T(8,128)S(1)}, u32[]{:S(2)}, u32[]{:S(2)}) %collective-permute-start.6) | collective-permute-done | bytes 163872 | tf_op jit(solution)/shard_map/ppermute | solution.py:552
  39.9 1.2 %place_stage.1 = f32[1280,256]{1,0:T(8,128)} custom-call(s32[1]{0:T(128)} %bitcast.8.where_ref, f32[320,128]{1,0:T(8,128)S(1)} %gain_stage.1.refs_0_, f32[320,128]{1,0:T(8,128)S(1)} %collective-permute-done.refs_1_, f32[320,128]{1,0:T(8,128)S(1)} %collective-permute-done.2.refs_2_, f32[320,128]{1,0:T(8,128)S(1)} %collective-permute-done.1.refs_3_, ...), custom_call_target="tpu_custom_call" | custom-call | tf_op jit(solution)/shard_map/place_stage/pallas_call | solution.py:476
Async XLA Ops:
  4.8 18.5 %all-to-all-start = ((f32[16,5,8,128]{3,2,1,0:T(8,128)}), f32[16,5,8,128]{3,2,1,0:T(8,128)S(1)}, u32[]{:S(2)}, u32[]{:S(2)}) async-start(f32[16,5,8,128]{3,2,1,0:T(8,128)} %get-tuple-element.18), calls=%async_computation | async-start | bytes 655360 | tf_op jit(solution)/shard_map/all_to_all | solution.py:533
  27.4 5.7 %collective-permute-start = (f32[320,128]{1,0:T(8,128)S(1)}, f32[320,128]{1,0:T(8,128)S(1)}, u32[]{:S(2)}, u32[]{:S(2)}) collective-permute-start(f32[320,128]{1,0:T(8,128)S(1)} %gain_stage.1.refs_0_), channel_id=1, source_target_pairs={{0,4},{1,3},{2,6},{3,1},{4,0},{5,7},{6,2},{7,5},{8,12},{9,11},{10,... | collective-permute-start | bytes 491528 | tf_op jit(solution)/shard_map/ppermute | solution.py:552
  29.5 6.2 %collective-permute-start.2 = (f32[320,128]{1,0:T(8,128)S(1)}, f32[320,128]{1,0:T(8,128)S(1)}, u32[]{:S(2)}, u32[]{:S(2)}) collective-permute-start(f32[320,128]{1,0:T(8,128)S(1)} %gain_stage.1.refs_0_), channel_id=1, source_target_pairs={{0,2},{1,5},{2,0},{3,7},{4,6},{5,1},{6,4},{7,3},{8,10},{9,13},{10,... | collective-permute-start | bytes 491528 | tf_op jit(solution)/shard_map/ppermute | solution.py:552
  33.2 5.3 %collective-permute-start.1 = (f32[320,128]{1,0:T(8,128)S(1)}, f32[320,128]{1,0:T(8,128)S(1)}, u32[]{:S(2)}, u32[]{:S(2)}) collective-permute-start(f32[320,128]{1,0:T(8,128)S(1)} %collective-permute-done.refs_1_), channel_id=1, source_target_pairs={{0,2},{1,5},{2,0},{3,7},{4,6},{5,1},{6,4},{7,3},{8,10},{9,13},{10,... | collective-permute-start | bytes 491528 | tf_op jit(solution)/shard_map/ppermute | solution.py:552
  33.2 5.3 %collective-permute-start.3 = (f32[320,128]{1,0:T(8,128)S(1)}, f32[320,128]{1,0:T(8,128)S(1)}, u32[]{:S(2)}, u32[]{:S(2)}) collective-permute-start(f32[320,128]{1,0:T(8,128)S(1)} %gain_stage.1.refs_0_), channel_id=1, source_target_pairs={{0,1},{1,0},{2,3},{3,2},{4,5},{5,4},{6,7},{7,6},{8,9},{9,8},{10,11... | collective-permute-start | bytes 491528 | tf_op jit(solution)/shard_map/ppermute | solution.py:552
  35.7 2.8 %collective-permute-start.4 = (f32[320,128]{1,0:T(8,128)S(1)}, f32[320,128]{1,0:T(8,128)S(1)}, u32[]{:S(2)}, u32[]{:S(2)}) collective-permute-start(f32[320,128]{1,0:T(8,128)S(1)} %collective-permute-done.refs_1_), channel_id=1, source_target_pairs={{0,1},{1,0},{2,3},{3,2},{4,5},{5,4},{6,7},{7,6},{8,9},{9,8},{10,11... | collective-permute-start | bytes 491528 | tf_op jit(solution)/shard_map/ppermute | solution.py:552
  36.2 2.3 %collective-permute-start.5 = (f32[320,128]{1,0:T(8,128)S(1)}, f32[320,128]{1,0:T(8,128)S(1)}, u32[]{:S(2)}, u32[]{:S(2)}) collective-permute-start(f32[320,128]{1,0:T(8,128)S(1)} %collective-permute-done.2.refs_2_), channel_id=1, source_target_pairs={{0,1},{1,0},{2,3},{3,2},{4,5},{5,4},{6,7},{7,6},{8,9},{9,8},{10,11... | collective-permute-start | bytes 491528 | tf_op jit(solution)/shard_map/ppermute | solution.py:552
  38.5 1.4 %collective-permute-start.6 = (f32[320,128]{1,0:T(8,128)S(1)}, f32[320,128]{1,0:T(8,128)S(1)}, u32[]{:S(2)}, u32[]{:S(2)}) collective-permute-start(f32[320,128]{1,0:T(8,128)S(1)} %collective-permute-done.1.refs_3_), channel_id=1, source_target_pairs={{0,1},{1,0},{2,3},{3,2},{4,5},{5,4},{6,7},{7,6},{8,9},{9,8},{10,11... | collective-permute-start | bytes 491528 | tf_op jit(solution)/shard_map/ppermute | solution.py:552

commit v6 on v5

--- a/solution.py
+++ b/solution.py
@@ -4,6 +4,7 @@
 from jax.experimental import pallas as pl
 from jax.experimental.pallas import tpu as pltpu
 from jax.sharding import PartitionSpec as P
+
 
 B = 256
 LANES = 128
@@ -102,7 +103,7 @@
         grad_ref, hess_ref, packet_ref = refs[8:11]
         square, chosen_ref = refs[11:13]
         copied = refs[13:21]
-        arrived, hot_ref = refs[21:23]
+        arrived = refs[21]
         bins_here, leaf_ref, score_ref, level_ref, rank_ref, length_ref, votes_ref, elected_ref = (
             copied
         )
@@ -147,19 +148,15 @@
         shared = jnp.where(lane < starts[-1], shared, 0.0)
         count = jnp.zeros((1, LANES), jnp.float32) + starts[-1].astype(jnp.float32)
         feature = lax.broadcasted_iota(jnp.int32, (padded, features), 1).astype(jnp.float32)
-        for first in range(0, leaves, group):
-            hot = []
-            for l in range(first, first + group):
-                hot.append((elected_t[0:padded, l : l + 1] == feature).astype(jnp.float32))
-            hot_ref[first * padded : (first + group) * padded, :] = jnp.concatenate(
-                hot, axis=0
-            ).astype(jnp.bfloat16)
         for fetch in fetches:
             fetch.wait()
         table = bins_here[...].astype(jnp.float32).astype(jnp.bfloat16)
         chosen = jnp.zeros((padded, documents), jnp.float32)
         for first in range(0, leaves, group):
-            hot = hot_ref[first * padded : (first + group) * padded, :]
+            hot = []
+            for l in range(first, first + group):
+                hot.append((elected_t[0:padded, l : l + 1] == feature).astype(jnp.float32))
+            hot = jnp.concatenate(hot, axis=0).astype(jnp.bfloat16)
             found = jnp.dot(hot, table, preferred_element_type=jnp.float32)
             for i in range(group):
                 chosen = jnp.where(
@@ -215,38 +212,40 @@
             pltpu.VMEM(votes.shape, jnp.int32),
             pltpu.VMEM(elected.shape, jnp.int32),
             pltpu.SemaphoreType.DMA((len(cuts) + 7,)),
-            pltpu.VMEM((leaves * padded, features), jnp.bfloat16),
         ],
         compiler_params=pltpu.CompilerParams(vmem_limit_bytes=48 << 20),
         name="local_stage",
     )(*[in_hbm(x) for x in (bins, leaf, score, level, rank, lengths, votes, elected)])
 
 
-def gain_stage(packets, where, leaves, plan):
+def gain_stage(packets, where, leaves, low, high, earlier, plan):
     devices = packets.shape[0]
     picks = plan["picks"]
-    units = plan["units"]
+    units = high - low
     chunks = plan["chunks"]
     chunk = 4 if devices % 4 == 0 else 1
-    even = units % HALVES == 0
+    even = plan["units"] % HALVES == 0
 
     half = cdiv(chunks, 2)
     batch = 4
 
-    def body(where_ref, packet_ref, out_ref, total_ref, grad_ref, hess_ref, late_ref):
+    def body(where_ref, packet_ref, *refs):
+        total_ref, grad_ref, hess_ref, late_ref = refs[-4:]
+        out_ref = refs[len(before)]
         leaf_id = lax.broadcasted_iota(jnp.int32, (leaves, LANES), 0).astype(jnp.float32)
         bin_id = lax.broadcasted_iota(jnp.int32, (LANES, LANES), 0).astype(jnp.float32)
         local = []
         limit = []
-        base = where_ref[0] % plan["owners"] * units
+        base = where_ref[0] % plan["owners"] * plan["units"]
         first = jnp.minimum(base // HALVES, plan["padded"] - picks)
-        for i in range(units):
+        for i in range(low, high):
             if even:
                 local.append(i // HALVES)
                 limit.append(bin_id + float(i % HALVES * LANES))
             else:
                 local.append(jnp.clip((base + i) // HALVES - first, 0, picks - 1))
                 limit.append(bin_id + ((base + i) % HALVES * LANES).astype(jnp.float32))
+
         def terms(tiles):
             weights = []
             steps = [[] for _ in range(units)]
@@ -341,13 +340,21 @@
         )
         for i in range(units):
             out_ref[i * leaves : (i + 1) * leaves, :] = gains[:, i * LANES : (i + 1) * LANES]
-
+        if before:
+            whole_ref = refs[len(before) + 1]
+            whole_ref[0 : low * leaves, :] = refs[0][...]
+            whole_ref[low * leaves :, :] = out_ref[...]
+
+    before = [] if earlier is None else [in_vmem(earlier)]
+    shapes = [vmem_array((units * leaves, LANES))]
+    if before:
+        shapes.append(vmem_array((high * leaves, LANES)))
     vmem = pl.BlockSpec(memory_space=pltpu.VMEM)
     return pl.pallas_call(
         body,
-        in_specs=[pl.BlockSpec(memory_space=pltpu.SMEM), vmem],
-        out_specs=vmem,
-        out_shape=vmem_array((units * leaves, LANES)),
+        in_specs=[pl.BlockSpec(memory_space=pltpu.SMEM), vmem] + [vmem] * len(before),
+        out_specs=[vmem] * len(shapes),
+        out_shape=shapes,
         scratch_shapes=[
             pltpu.VMEM((4 * leaves, units * LANES), jnp.float32),
             pltpu.VMEM((leaves, LANES), jnp.float32),
@@ -356,15 +363,15 @@
         ],
         compiler_params=pltpu.CompilerParams(vmem_limit_bytes=48 << 20),
         name="gain_stage",
-    )(where, in_vmem(packets))
-
-
-def vote_stage(packets, before, sources, features, leaves, kept, plan):
+    )(where, in_vmem(packets), *before)
+
+
+def vote_stage(packets, before, sources, last, features, leaves, kept, plan):
     rows = plan["rows"]
     lines = plan["vote_lines"]
     step = 64
     depth = round_up(features, LANES)
-    last = before is not None
+    inputs = [in_vmem(packets)] + ([] if before is None else [in_vmem(before)])
 
     def body(packet_ref, *refs):
         out_ref, count = refs[-2:] if last else (None, refs[-1])
@@ -376,7 +383,7 @@
                 jnp.float32
             )
             total = jnp.zeros((step, LANES), jnp.float32)
-            if last:
+            if before is not None:
                 total = refs[0][pl.ds(start, step), :]
             for s in sources:
                 for line in range(lines):
@@ -399,11 +406,9 @@
 
     vmem = pl.BlockSpec(memory_space=pltpu.VMEM)
     if last:
-        inputs = [in_vmem(packets), in_vmem(before)]
         out_shape = jax.ShapeDtypeStruct((leaves, features), jnp.int32)
         scratch = [pltpu.VMEM((depth, LANES), jnp.float32)]
     else:
-        inputs = [in_vmem(packets)]
         out_shape = vmem_array((depth, LANES))
         scratch = []
     return pl.pallas_call(
@@ -418,7 +423,7 @@
     )(*inputs)
 
 
-def place_stage(blocks, where, leaves, picked, plan):
+def place_stage(blocks, tags, spans, where, leaves, picked, plan):
     units = plan["units"]
     owners = plan["owners"]
     step = 8 if leaves % 8 == 0 else leaves
@@ -435,24 +440,25 @@
             if not plan["doubling"]:
                 owner.append(index)
                 continue
-            even_tag, odd_tag = plan["tags"][index % len(plan["tags"])]
-            if index < len(plan["tags"]):
+            even_tag, odd_tag = tags[index][0:2]
+            if not tags[index][2]:
                 owner.append(here ^ jnp.where(odd == 1, odd_tag, even_tag))
             else:
                 owner.append(here ^ 1 ^ jnp.where(odd == 1, even_tag, odd_tag))
         copies = []
         for g in range(groups):
             for index, ref in enumerate(refs[:-3]):
-                for i in range(units):
-
-                    def write(index=index, ref=ref, i=i):
+                low, high = spans[index]
+                for i in range(low, high):
+
+                    def write(index=index, ref=ref, i=i, low=low):
                         if units % HALVES == 0:
                             half = i % HALVES
                             pick = owner[index] * (units // HALVES) + i // HALVES
                         else:
                             half = (owner[index] * units + i) % HALVES
                             pick = (owner[index] * units + i) // HALVES
-                        start = i * leaves + g * step
+                        start = (i - low) * leaves + g * step
                         planes[half, pl.ds(g * rows + pick, step, stride=picked), :] = ref[
                             start : start + step, :
                         ]
@@ -499,7 +505,7 @@
         kept = feature_votes.shape[2]
         doubling = devices >= 8 and devices & (devices - 1) == 0
         owners = devices // 2 if doubling else devices
-        units = cdiv(picked * HALVES, owners)
+        units = max(cdiv(picked * HALVES, owners), 2)
         padded = round_up(picked, 8)
         picks = max(
             (j * units + units - 1) // HALVES - (j * units) // HALVES + 1 for j in range(owners)
@@ -531,10 +537,15 @@
             plan,
         )
         received = lax.all_to_all(packets, "rows", 0, 0)
-        block = gain_stage(received, where, leaves, plan)
-        middle = cdiv(devices, 2)
-        count_args = (features, leaves, kept, plan)
-        votes = vote_stage(received, None, range(middle), *count_args)
+        counters = (features, leaves, kept, plan)
+        third = cdiv(devices, 3)
+        shares = [range(min(k * third, devices), min((k + 1) * third, devices)) for k in range(3)]
+        cut = units * 3 // 5
+        if units % HALVES == 0:
+            cut = max(cut // HALVES, 1) * HALVES if units > HALVES else 1
+        (part,) = gain_stage(received, where, leaves, 0, cut, None, plan)
+        rest, block = gain_stage(received, where, leaves, cut, units, part, plan)
+        votes = vote_stage(received, None, shares[0], False, *counters)
         if doubling:
             far = [1 << b for b in reversed(range(1, owners.bit_length() - 1))]
             twin = list(far)
@@ -543,38 +554,59 @@
                 [(i, i ^ (twin[p] if i & 1 else far[p])) for i in range(devices)]
                 for p in range(len(far))
             ]
-            tags = [(0, 0)]
-            for p in range(len(far)):
-                tags = tags + [(even | far[p], odd | twin[p]) for even, odd in tags]
             sibling = [(i, i ^ 1) for i in range(devices)]
 
-            def send(b, pair):
-                return lax.ppermute(b, "rows", pair)
-
-            moved = send(block, pairs[0])
-            again, votes = lax.optimization_barrier((block, votes))
-            crossed = [send(again, sibling)]
-            moved, votes = lax.optimization_barrier((moved, votes))
-            blocks = [block, moved]
+            def send(items, p):
+                return [
+                    (lax.ppermute(b, "rows", pairs[p]), even ^ far[p], odd ^ twin[p], low, high)
+                    for b, even, odd, low, high in items
+                ]
+
+            def cross(items):
+                return [(lax.ppermute(item[0], "rows", sibling),) + item[1:] for item in items]
+
+            def after(items, other):
+                arrays, other = lax.optimization_barrier(([item[0] for item in items], other))
+                return [(b,) + item[1:] for b, item in zip(arrays, items)], other
+
+            own = [(block, 0, 0, 0, units)]
+            first = send([(part, 0, 0, 0, cut)], 0)
+            second = send([(rest, 0, 0, cut, units)], 0)
+            crossed = cross(own)
+            first, votes = after(first, votes)
+            votes = vote_stage(received, votes, shares[1], False, *counters)
+            second, votes = after(second, votes)
+            votes = vote_stage(received, votes, shares[2], True, *counters)
+            items = own + first + second
             for p in range(1, len(far)):
-                moved = [send(b, pairs[p]) for b in [again] + blocks[1:]]
-                if p == len(far) - 1:
-                    votes = vote_stage(received, votes, range(middle, devices), *count_args)
-                    waiting, votes = lax.optimization_barrier((blocks[1:] + moved[:-1], votes))
-                    crossed = crossed + [send(b, sibling) for b in waiting]
-                    moved[-1], votes = lax.optimization_barrier((moved[-1], votes))
-                blocks = blocks + moved
+                if p < len(far) - 1:
+                    items = items + send(items, p)
+                    continue
+                moved = send(own, p)
+                moved = moved + send(items[1:-1], p)
+                moved = moved + send(items[-1:], p)
+                crossed = crossed + cross(items[1:] + moved[:-2])
+                crossed = crossed + cross(moved[-2:-1])
+                crossed[-3:], joint = after(crossed[-3:], (moved[-1][0], votes))
+                moved[-1] = (joint[0],) + moved[-1][1:]
+                votes = joint[1]
+                crossed = crossed + cross(moved[-1:])
+                items = items + moved
             if len(far) == 1:
-                votes = vote_stage(received, votes, range(middle, devices), *count_args)
-            blocks = blocks + crossed + [send(blocks[-1], sibling)]
-            plan["tags"] = tags
+                crossed = crossed + cross(items[1:])
+            tags = [item[1:3] + (False,) for item in items]
+            tags = tags + [item[1:3] + (True,) for item in crossed]
+            spans = [item[3:5] for item in items + crossed]
+            blocks = [item[0] for item in items + crossed]
         else:
-            votes = vote_stage(received, votes, range(middle, devices), *count_args)
+            votes = vote_stage(received, votes, range(third, devices), True, *counters)
             gathered = lax.all_gather(block, "rows", axis=0)
             blocks = [gathered[j] for j in range(devices)]
-            plan["tags"] = None
-        split_gain = place_stage(blocks, where, leaves, picked, plan)
+            tags = None
+            spans = [(0, units)] * devices
+        split_gain = place_stage(blocks, tags, spans, where, leaves, picked, plan)
         return gradient.reshape(-1), hessian.reshape(-1), votes, split_gain
+
 
     return jax.shard_map(
         on_device,

time: 41.3 us -> 47.3 us (1.15)
  starting transfers between devices: 9.48 us -> 12.6 us
  waiting for transfers between devices: 17.1 us -> 20 us
    ppermute x7 -> x11, starting transfers between devices: 2.05 us -> 5.14 us  [the longest x5 4.05 us: send(): lax.ppermute(b, 'rows', pairs[p])]
    ppermute x7 -> x11, waiting for transfers between devices: 6.05 us -> 8.9 us  [the longest x5 7.99 us: send(): lax.ppermute(b, 'rows', pairs[p])]
    pallas_call x1 -> x2, Pallas kernels: 4.12 us -> 4.37 us  [gain_stage(): pl.pallas_call(body, in_specs=[pl.BlockSpec(memory_space=pltpu.SMEM), vme...]
    pallas_call x2 -> x3, Pallas kernels: 4.33 us -> 4.41 us  [vote_stage(): pl.pallas_call(body, in_specs=[vmem] * len(inputs), out_specs=vmem, out_s...]
  transfers between devices with their start and end apart: 8 -> 12, of which waited for: 4 -> 5; matrix products, arithmetic and copies ran while one was open for 0% -> 0% of each run, Pallas kernels for 11% -> 9%
where the time goes in v6:
time: 47.3 us; the launch traced here: 47 us
  waiting for transfers between devices  20 us (42%)
  Pallas kernels  13.8 us (29%)
  starting transfers between devices  12.6 us (27%)
  between operations  0.69 us (1%)
    all_to_all x1, waiting for transfers between devices, on_device(): received = lax.all_to_all(packets, 'rows', 0, 0)  11.1 us
    ppermute x5, waiting for transfers between devices, send(): lax.ppermute(b, 'rows', pairs[p])  7.99 us
    all_to_all x1, starting transfers between devices, on_device(): received = lax.all_to_all(packets, 'rows', 0, 0)  7.43 us
    pallas_call x3, Pallas kernels, vote_stage(): pl.pallas_call(body, in_specs=[vmem] * len(inputs), out_specs=vmem, out_s...  4.41 us
    pallas_call x2, Pallas kernels, gain_stage(): pl.pallas_call(body, in_specs=[pl.BlockSpec(memory_space=pltpu.SMEM), vme...  4.37 us
    ppermute x5, starting transfers between devices, send(): lax.ppermute(b, 'rows', pairs[p])  4.05 us
    pallas_call x1, Pallas kernels, local_stage(): pl.pallas_call(body, in_specs=[pl.BlockSpec(memory_space=pltpu.HBM)] * 8,...  3.86 us
    pallas_call x1, Pallas kernels, place_stage(): pl.pallas_call(body, in_specs=[pl.BlockSpec(memory_space=pltpu.SMEM)] + [...  1.19 us
  transfers between devices with their start and end apart: 12, of which 5 were waited for; matrix products, arithmetic and copies ran while one was open for 0% of the time, Pallas kernels for 9%

profile of v6, /device:TPU:0, one launch (start us, length us, event | category | flops | bytes accessed | tf_op | source)
XLA Modules:
  0.0 47.0 jit_solution(1258563158590124815)
XLA Ops:
  0.6 3.9 %local_stage.1 = (f32[1,512]{1,0:T(1,128)}, f32[1,512]{1,0:T(1,128)}, f32[16,5,8,128]{3,2,1,0:T(8,128)}) custom-call(s32[700,512]{1,0:T(8,128)} %bitcast.10, s32[1,512]{1,0:T(1,128)} %bitcast.13, f32[1,512]{1,0:T(1,128)} %bitcast.14, s32[1,512]{1,0:T(1,128)} %bitcast.15, s32[1,512]{1,0:T(1,128)} %bitcast.16, s32[2]{0:T(128)} %refs_5_.1, ...), custom_call_target="tpu_custom_call" | custom-call | tf_op jit(solution)/shard_map/local_stage/pallas_call | solution.py:192
  4.5 7.4 %all-to-all-start = ((f32[16,5,8,128]{3,2,1,0:T(8,128)}), f32[16,5,8,128]{3,2,1,0:T(8,128)S(1)}, u32[]{:S(2)}, u32[]{:S(2)}) async-start(f32[16,5,8,128]{3,2,1,0:T(8,128)} %get-tuple-element.20), calls=%async_computation | async-start | bytes 655360 | tf_op jit(solution)/shard_map/all_to_all | solution.py:539
  11.9 11.1 %all-to-all-done.packet_ref = f32[16,5,8,128]{3,2,1,0:T(8,128)S(1)} async-done(((f32[16,5,8,128]{3,2,1,0:T(8,128)}), f32[16,5,8,128]{3,2,1,0:T(8,128)S(1)}, u32[]{:S(2)}, u32[]{:S(2)}) %all-to-all-start) | async-done | bytes 327712 | tf_op jit(solution)/shard_map/all_to_all | solution.py:539
  23.0 2.6 %gain_stage.2.refs_0_ = f32[192,128]{1,0:T(8,128)S(1)} custom-call(s32[1]{0:T(128)} %bitcast.8.where_ref, f32[16,5,8,128]{3,2,1,0:T(8,128)S(1)} %all-to-all-done.packet_ref), custom_call_target="tpu_custom_call" | custom-call | tf_op jit(solution)/shard_map/gain_stage/pallas_call | solution.py:353
  25.6 1.8 %gain_stage.3 = (f32[128,128]{1,0:T(8,128)S(1)}, f32[320,128]{1,0:T(8,128)S(1)}) custom-call(s32[1]{0:T(128)} %bitcast.8.where_ref, f32[16,5,8,128]{3,2,1,0:T(8,128)S(1)} %all-to-all-done.packet_ref, f32[192,128]{1,0:T(8,128)S(1)} %gain_stage.2.refs_0_), custom_call_target="tpu_custom_call" | custom-call | tf_op jit(solution)/shard_map/gain_stage/pallas_call | solution.py:353
  27.4 0.1 collective-permute-start.3
  27.5 1.4 %collective-permute-start.1 = (f32[192,128]{1,0:T(8,128)S(1)}, f32[192,128]{1,0:T(8,128)S(1)}, u32[]{:S(2)}, u32[]{:S(2)}) collective-permute-start(f32[192,128]{1,0:T(8,128)S(1)} %gain_stage.2.refs_0_), channel_id=1, source_target_pairs={{0,4},{1,3},{2,6},{3,1},{4,0},{5,7},{6,2},{7,5},{8,12},{9,11},{10,... | collective-permute-start | bytes 294920 | tf_op jit(solution)/shard_map/ppermute | solution.py:561
  28.9 1.3 %vote_stage.3.refs_0_ = f32[768,128]{1,0:T(8,128)S(1)} custom-call(f32[16,5,8,128]{3,2,1,0:T(8,128)S(1)} %all-to-all-done.packet_ref), custom_call_target="tpu_custom_call" | custom-call | flops 20000000 | bytes 400000 | tf_op jit(solution)/shard_map/vote_stage/pallas_call | solution.py:414
  30.2 2.8 %collective-permute-done.1.refs_1_ = f32[192,128]{1,0:T(8,128)S(1)} collective-permute-done((f32[192,128]{1,0:T(8,128)S(1)}, f32[192,128]{1,0:T(8,128)S(1)}, u32[]{:S(2)}, u32[]{:S(2)}) %collective-permute-start.1) | collective-permute-done | bytes 98336 | tf_op jit(solution)/shard_map/ppermute | solution.py:561
  33.0 1.1 %collective-permute-start.5 = (f32[192,128]{1,0:T(8,128)S(1)}, f32[192,128]{1,0:T(8,128)S(1)}, u32[]{:S(2)}, u32[]{:S(2)}) collective-permute-start(f32[192,128]{1,0:T(8,128)S(1)} %collective-permute-done.1.refs_1_), channel_id=1, source_target_pairs={{0,2},{1,5},{2,0},{3,7},{4,6},{5,1},{6,4},{7,3},{8,10},{9,13},{10,... | collective-permute-start | bytes 294920 | tf_op jit(solution)/shard_map/ppermute | solution.py:561
  34.1 0.6 %collective-permute-start = (f32[128,128]{1,0:T(8,128)S(1)}, f32[128,128]{1,0:T(8,128)S(1)}, u32[]{:S(2)}, u32[]{:S(2)}) collective-permute-start(f32[128,128]{1,0:T(8,128)S(1)} %get-tuple-element.21), channel_id=1, source_target_pairs={{0,4},{1,3},{2,6},{3,1},{4,0},{5,7},{6,2},{7,5},{8,12},{9,11},{10,... | collective-permute-start | bytes 196616 | tf_op jit(solution)/shard_map/ppermute | solution.py:561
  34.7 0.0 collective-permute-done.3.refs_3_
  34.7 0.0 collective-permute-start.4
  34.7 0.5 %collective-permute-start.8 = (f32[320,128]{1,0:T(8,128)S(1)}, f32[320,128]{1,0:T(8,128)S(1)}, u32[]{:S(2)}, u32[]{:S(2)}) collective-permute-start(f32[320,128]{1,0:T(8,128)S(1)} %get-tuple-element.24.refs_0_), channel_id=1, source_target_pairs={{0,1},{1,0},{2,3},{3,2},{4,5},{5,4},{6,7},{7,6},{8,9},{9,8},{10,11... | collective-permute-start | bytes 491528 | tf_op jit(solution)/shard_map/ppermute | solution.py:566
  35.2 1.3 %vote_stage.4.refs_0_ = f32[768,128]{1,0:T(8,128)S(1)} custom-call(f32[16,5,8,128]{3,2,1,0:T(8,128)S(1)} %all-to-all-done.packet_ref, f32[768,128]{1,0:T(8,128)S(1)} %vote_stage.3.refs_0_), custom_call_target="tpu_custom_call" | custom-call | flops 20000000 | bytes 400000 | tf_op jit(solution)/shard_map/vote_stage/pallas_call | solution.py:414
  36.5 1.9 %collective-permute-done.refs_2_ = f32[128,128]{1,0:T(8,128)S(1)} collective-permute-done((f32[128,128]{1,0:T(8,128)S(1)}, f32[128,128]{1,0:T(8,128)S(1)}, u32[]{:S(2)}, u32[]{:S(2)}) %collective-permute-start) | collective-permute-done | bytes 65568 | tf_op jit(solution)/shard_map/ppermute | solution.py:561
  38.4 0.0 collective-permute-done.5.refs_4_
  38.4 0.0 collective-permute-start.6
  38.4 0.9 %collective-permute-start.7 = (f32[128,128]{1,0:T(8,128)S(1)}, f32[128,128]{1,0:T(8,128)S(1)}, u32[]{:S(2)}, u32[]{:S(2)}) collective-permute-start(f32[128,128]{1,0:T(8,128)S(1)} %collective-permute-done.refs_2_), channel_id=1, source_target_pairs={{0,2},{1,5},{2,0},{3,7},{4,6},{5,1},{6,4},{7,3},{8,10},{9,13},{10,... | collective-permute-start | bytes 196616 | tf_op jit(solution)/shard_map/ppermute | solution.py:561
  39.3 0.0 collective-permute-start.2
  39.3 3.4 %collective-permute-done.7.refs_5_ = f32[128,128]{1,0:T(8,128)S(1)} collective-permute-done((f32[128,128]{1,0:T(8,128)S(1)}, f32[128,128]{1,0:T(8,128)S(1)}, u32[]{:S(2)}, u32[]{:S(2)}) %collective-permute-start.7) | collective-permute-done | bytes 65568 | tf_op jit(solution)/shard_map/ppermute | solution.py:561
  42.6 0.0 collective-permute-start.9
  42.6 1.7 %vote_stage.5 = s32[32,700]{1,0:T(8,128)} custom-call(f32[16,5,8,128]{3,2,1,0:T(8,128)S(1)} %all-to-all-done.packet_ref, f32[768,128]{1,0:T(8,128)S(1)} %vote_stage.4.refs_0_), custom_call_target="tpu_custom_call" | custom-call | flops 20000000 | bytes 400000 | tf_op jit(solution)/shard_map/vote_stage/pallas_call | solution.py:414
  44.4 0.0 collective-permute-done.2.refs_8_
  44.4 0.0 collective-permute-done.6.refs_10_
  44.4 0.0 collective-permute-done.4.refs_9_
  44.4 0.6 %collective-permute-start.10 = (f32[128,128]{1,0:T(8,128)S(1)}, f32[128,128]{1,0:T(8,128)S(1)}, u32[]{:S(2)}, u32[]{:S(2)}) collective-permute-start(f32[128,128]{1,0:T(8,128)S(1)} %collective-permute-done.7.refs_5_), channel_id=1, source_target_pairs={{0,1},{1,0},{2,3},{3,2},{4,5},{5,4},{6,7},{7,6},{8,9},{9,8},{10,11... | collective-permute-start | bytes 196616 | tf_op jit(solution)/shard_map/ppermute | solution.py:566
  45.0 0.0 collective-permute-done.8.refs_6_
  45.0 0.0 collective-permute-done.9.refs_7_
  45.0 0.9 %collective-permute-done.10.refs_11_ = f32[128,128]{1,0:T(8,128)S(1)} collective-permute-done((f32[128,128]{1,0:T(8,128)S(1)}, f32[128,128]{1,0:T(8,128)S(1)}, u32[]{:S(2)}, u32[]{:S(2)}) %collective-permute-start.10) | collective-permute-done | bytes 65568 | tf_op jit(solution)/shard_map/ppermute | solution.py:566
  45.9 1.2 %place_stage.1 = f32[1280,256]{1,0:T(8,128)} custom-call(s32[1]{0:T(128)} %bitcast.8.where_ref, f32[320,128]{1,0:T(8,128)S(1)} %get-tuple-element.24.refs_0_, f32[192,128]{1,0:T(8,128)S(1)} %collective-permute-done.1.refs_1_, f32[128,128]{1,0:T(8,128)S(1)} %collective-permute-done.refs_2_, f32[320,128]{1,0:T(8,128)S(1)} %collective-permute-done.3.refs_3_, ...), custom_call_target="tpu_custom_call" | custom-call | tf_op jit(solution)/shard_map/place_stage/pallas_call | solution.py:482
Async XLA Ops:
  4.5 18.5 %all-to-all-start = ((f32[16,5,8,128]{3,2,1,0:T(8,128)}), f32[16,5,8,128]{3,2,1,0:T(8,128)S(1)}, u32[]{:S(2)}, u32[]{:S(2)}) async-start(f32[16,5,8,128]{3,2,1,0:T(8,128)} %get-tuple-element.20), calls=%async_computation | async-start | bytes 655360 | tf_op jit(solution)/shard_map/all_to_all | solution.py:539
  27.4 7.3 %collective-permute-start.3 = (f32[320,128]{1,0:T(8,128)S(1)}, f32[320,128]{1,0:T(8,128)S(1)}, u32[]{:S(2)}, u32[]{:S(2)}) collective-permute-start(f32[320,128]{1,0:T(8,128)S(1)} %get-tuple-element.24.refs_0_), channel_id=1, source_target_pairs={{0,2},{1,5},{2,0},{3,7},{4,6},{5,1},{6,4},{7,3},{8,10},{9,13},{10,... | collective-permute-start | bytes 491528 | tf_op jit(solution)/shard_map/ppermute | solution.py:561
  27.5 5.5 %collective-permute-start.1 = (f32[192,128]{1,0:T(8,128)S(1)}, f32[192,128]{1,0:T(8,128)S(1)}, u32[]{:S(2)}, u32[]{:S(2)}) collective-permute-start(f32[192,128]{1,0:T(8,128)S(1)} %gain_stage.2.refs_0_), channel_id=1, source_target_pairs={{0,4},{1,3},{2,6},{3,1},{4,0},{5,7},{6,2},{7,5},{8,12},{9,11},{10,... | collective-permute-start | bytes 294920 | tf_op jit(solution)/shard_map/ppermute | solution.py:561
  33.0 5.4 %collective-permute-start.5 = (f32[192,128]{1,0:T(8,128)S(1)}, f32[192,128]{1,0:T(8,128)S(1)}, u32[]{:S(2)}, u32[]{:S(2)}) collective-permute-start(f32[192,128]{1,0:T(8,128)S(1)} %collective-permute-done.1.refs_1_), channel_id=1, source_target_pairs={{0,2},{1,5},{2,0},{3,7},{4,6},{5,1},{6,4},{7,3},{8,10},{9,13},{10,... | collective-permute-start | bytes 294920 | tf_op jit(solution)/shard_map/ppermute | solution.py:561
  34.1 4.3 %collective-permute-start = (f32[128,128]{1,0:T(8,128)S(1)}, f32[128,128]{1,0:T(8,128)S(1)}, u32[]{:S(2)}, u32[]{:S(2)}) collective-permute-start(f32[128,128]{1,0:T(8,128)S(1)} %get-tuple-element.21), channel_id=1, source_target_pairs={{0,4},{1,3},{2,6},{3,1},{4,0},{5,7},{6,2},{7,5},{8,12},{9,11},{10,... | collective-permute-start | bytes 196616 | tf_op jit(solution)/shard_map/ppermute | solution.py:561
  34.7 9.7 %collective-permute-start.4 = (f32[320,128]{1,0:T(8,128)S(1)}, f32[320,128]{1,0:T(8,128)S(1)}, u32[]{:S(2)}, u32[]{:S(2)}) collective-permute-start(f32[320,128]{1,0:T(8,128)S(1)} %collective-permute-done.3.refs_3_), channel_id=1, source_target_pairs={{0,1},{1,0},{2,3},{3,2},{4,5},{5,4},{6,7},{7,6},{8,9},{9,8},{10,11... | collective-permute-start | bytes 491528 | tf_op jit(solution)/shard_map/ppermute | solution.py:566
  34.7 10.3 %collective-permute-start.8 = (f32[320,128]{1,0:T(8,128)S(1)}, f32[320,128]{1,0:T(8,128)S(1)}, u32[]{:S(2)}, u32[]{:S(2)}) collective-permute-start(f32[320,128]{1,0:T(8,128)S(1)} %get-tuple-element.24.refs_0_), channel_id=1, source_target_pairs={{0,1},{1,0},{2,3},{3,2},{4,5},{5,4},{6,7},{7,6},{8,9},{9,8},{10,11... | collective-permute-start | bytes 491528 | tf_op jit(solution)/shard_map/ppermute | solution.py:566
  38.4 6.0 %collective-permute-start.6 = (f32[192,128]{1,0:T(8,128)S(1)}, f32[192,128]{1,0:T(8,128)S(1)}, u32[]{:S(2)}, u32[]{:S(2)}) collective-permute-start(f32[192,128]{1,0:T(8,128)S(1)} %collective-permute-done.5.refs_4_), channel_id=1, source_target_pairs={{0,1},{1,0},{2,3},{3,2},{4,5},{5,4},{6,7},{7,6},{8,9},{9,8},{10,11... | collective-permute-start | bytes 294920 | tf_op jit(solution)/shard_map/ppermute | solution.py:566
  38.4 4.3 %collective-permute-start.7 = (f32[128,128]{1,0:T(8,128)S(1)}, f32[128,128]{1,0:T(8,128)S(1)}, u32[]{:S(2)}, u32[]{:S(2)}) collective-permute-start(f32[128,128]{1,0:T(8,128)S(1)} %collective-permute-done.refs_2_), channel_id=1, source_target_pairs={{0,2},{1,5},{2,0},{3,7},{4,6},{5,1},{6,4},{7,3},{8,10},{9,13},{10,... | collective-permute-start | bytes 196616 | tf_op jit(solution)/shard_map/ppermute | solution.py:561
  39.3 5.1 %collective-permute-start.2 = (f32[128,128]{1,0:T(8,128)S(1)}, f32[128,128]{1,0:T(8,128)S(1)}, u32[]{:S(2)}, u32[]{:S(2)}) collective-permute-start(f32[128,128]{1,0:T(8,128)S(1)} %collective-permute-done.refs_2_), channel_id=1, source_target_pairs={{0,1},{1,0},{2,3},{3,2},{4,5},{5,4},{6,7},{7,6},{8,9},{9,8},{10,11... | collective-permute-start | bytes 196616 | tf_op jit(solution)/shard_map/ppermute | solution.py:566
  42.6 2.3 %collective-permute-start.9 = (f32[192,128]{1,0:T(8,128)S(1)}, f32[192,128]{1,0:T(8,128)S(1)}, u32[]{:S(2)}, u32[]{:S(2)}) collective-permute-start(f32[192,128]{1,0:T(8,128)S(1)} %collective-permute-done.1.refs_1_), channel_id=1, source_target_pairs={{0,1},{1,0},{2,3},{3,2},{4,5},{5,4},{6,7},{7,6},{8,9},{9,8},{10,11... | collective-permute-start | bytes 294920 | tf_op jit(solution)/shard_map/ppermute | solution.py:566
  44.4 1.5 %collective-permute-start.10 = (f32[128,128]{1,0:T(8,128)S(1)}, f32[128,128]{1,0:T(8,128)S(1)}, u32[]{:S(2)}, u32[]{:S(2)}) collective-permute-start(f32[128,128]{1,0:T(8,128)S(1)} %collective-permute-done.7.refs_5_), channel_id=1, source_target_pairs={{0,1},{1,0},{2,3},{3,2},{4,5},{5,4},{6,7},{7,6},{8,9},{9,8},{10,11... | collective-permute-start | bytes 196616 | tf_op jit(solution)/shard_map/ppermute | solution.py:566
